TPU v7x, 128 devices: a whole 4x4x4 slice. The times are simulated.
128 devices in a mesh: mkt: 32 (over x, z, core), grp: 4 (over y).
Axes of the slice: x: 4, y: 4, z: 4, core: 2. Of those that a mesh axis runs over, the one named last changes fastest.
Arguments:
- mean_utility: float32 [2048, 64], P(('mkt', 'grp')), may hold values from -5 to -1
- market_share: float32 [2048, 64], P(('mkt', 'grp')), may hold values from 0.001 to 0.02
- product_traits: float32 [2048, 64, 5], P(('mkt', 'grp')), may hold values from -1 to 1
- taste_draws: float32 [2048, 5, 1024], P(('mkt', 'grp')), may hold values from -4 to 4
- taste_scale: float32 [5], replicated, may hold values from 0.3 to 1
- type_weight: float32 [2048, 1024], P(('mkt', 'grp')), may hold values from 0.1 to 1
- market_size: float32 [2048], P(('mkt', 'grp')), may hold values from 0.05 to 3
- product_firm: int32 [2048, 64], P(('mkt', 'grp')), may hold values from 0 to 511, all different within a row
- firm_order: int32 [512], replicated, may hold values from 0 to 511, each once
- loyalty: float32 [512, 1024], P(('mkt', 'grp')), may hold values from -1 to 1
- firm_share: float32 [512, 1024], replicated, may hold values from 2e-05 to 0.15
Outputs:
- utility_out: float32 [2048, 64], P(('mkt', 'grp'))
- loyalty_out: float32 [512, 1024], P(('mkt', 'grp'))
Inputs may be any that keep to these rules, and one draw needn't show every extreme that they name: `product_firm`: in each market the 64 products belong to 64 different firms, and every firm sells in some market. `firm_order`: each firm appears once.
All inputs are finite; a program needn't handle non-finite values.
Results may differ from a plain program's by a relative error of at most 0.0001.
Values sent between devices are 32-bit elements; how exact they have to be, the bound alone decides.
A program may use at most 64 MiB of HBM per device.

v0:
```python
import jax
import jax.numpy as jnp
from jax import lax
from jax.sharding import Mesh
from jax.sharding import PartitionSpec as P

ITERS = 3
MKT_GRP = ("mkt_0", "mkt_1", "mkt_2", "grp")
MKT = ("mkt_0", "mkt_1", "mkt_2")


clip_target = 0.5
norm_eps = 1e-06


def sent_to_all(array, axis):
    copies = jnp.broadcast_to(array, (lax.axis_size(axis), *array.shape))
    return lax.all_to_all(copies, axis, split_axis=0, concat_axis=0, tiled=True)


def of_everyone(array, axis):
    return sent_to_all(array, axis).sum(axis=0)


def one_axis_at_a_time(array, axes):
    far, near = axes
    return of_everyone(of_everyone(array, near), far)


def joined_along(tiles, dim):
    tiles = jnp.moveaxis(tiles, 0, dim)
    lengths = tiles.shape
    return tiles.reshape(*lengths[:dim], lengths[dim] * lengths[dim + 1], *lengths[dim + 2 :])


def whole_of(array, axes, dim):
    far, near = axes
    leading = sent_to_all(array, far)
    tiles = jnp.swapaxes(sent_to_all(leading, near), 0, 1)
    return joined_along(tiles.reshape(-1, *array.shape), dim)


def split_up(array, dim, peers):
    lengths = array.shape
    tiles = array.reshape(*lengths[:dim], peers, lengths[dim] // peers, *lengths[dim + 1 :])
    return jnp.moveaxis(tiles, dim, 0)


def one_exchange(array, axis, axes, splits, concats):
    sizes = [lax.axis_size(a) for a in axes]
    tiles = split_up(array, splits[0], sizes[0])
    tiles = jnp.moveaxis(split_up(tiles, splits[1] + 1, sizes[1]), 0, 1)
    inside = tiles.shape[2:]
    tiles = tiles.reshape(-1, *inside)
    tiles = lax.all_to_all(tiles, axis, split_axis=0, concat_axis=0, tiled=True)
    tiles = joined_along(tiles.reshape(*sizes, *inside), concats[0] + 1)
    return joined_along(tiles, concats[1])


def inverse_order(firm_order):
    count = firm_order.shape[0]
    return jnp.zeros((count,), jnp.int32).at[firm_order].set(jnp.arange(count, dtype=jnp.int32))


def market_terms(mean_now, taste, type_weight, mass, row_ids, table):
    expu = jnp.exp(mean_now[:, :, None] + taste + jnp.take(table, row_ids, axis=0))
    choice_prob = expu / (1.0 + jnp.sum(expu, axis=1, keepdims=True))
    weighted_sum = jnp.einsum(
        "mjr,mr->mj", choice_prob, type_weight, precision=lax.Precision.HIGHEST
    )
    weighted = choice_prob * mass[:, None, :]
    firm_count = table.shape[0]
    onehot = (
        jnp.arange(firm_count, dtype=jnp.int32)[:, None] == row_ids.reshape(-1)[None, :]
    ).astype(jnp.float32)
    partial_value = jnp.dot(
        onehot,
        weighted.reshape(-1, weighted.shape[2]),
        precision=lax.Precision.HIGHEST,
        preferred_element_type=jnp.float32,
    )
    return (weighted_sum, partial_value)


def local(
    mean_utility,
    market_share,
    product_traits,
    taste_draws,
    taste_scale,
    type_weight,
    market_size,
    product_firm,
    firm_order,
    loyalty,
    firm_share,
):
    firm_count = firm_share.shape[0]
    draw_count = firm_share.shape[1]
    owned_count = loyalty.shape[0]
    inverse = inverse_order(firm_order)
    owner_rows = jnp.take(inverse, product_firm, axis=0)
    owned = loyalty
    my_firms = lax.dynamic_slice_in_dim(
        firm_order, lax.axis_index(MKT_GRP) * owned_count, owned_count
    )
    taste = jnp.einsum(
        "mjk,mkr->mjr", product_traits * taste_scale, taste_draws, precision=lax.Precision.HIGHEST
    )
    weight_total = jnp.sum(type_weight, axis=1)
    mass = market_size[:, None] * type_weight
    type_mass = one_axis_at_a_time(jnp.sum(mass, axis=0), (("mkt_0", "mkt_1"), ("mkt_2", "grp")))
    log_observed = jnp.log(market_share)
    mean_now = mean_utility
    my_share = jnp.log(jnp.take(firm_share, my_firms, axis=0))
    for step in range(ITERS):
        table = whole_of(owned, (("mkt_0", "mkt_1"), ("mkt_2", "grp")), 0)
        weighted_sum, by_owner = market_terms(mean_now, taste, type_weight, mass, owner_rows, table)
        predicted = weighted_sum / weight_total[:, None]
        blocks = by_owner.reshape(lax.axis_size(MKT), lax.axis_size("grp"), owned_count, draw_count)
        received = one_exchange(blocks, MKT_GRP, (MKT, "grp"), (0, 1), (0, 1))
        own_totals = jnp.sum(received, axis=(0, 1))
        gap = my_share - jnp.log(own_totals / type_mass[None, :])
        squares = one_axis_at_a_time(jnp.sum(gap * gap), (("mkt_0", "mkt_1"), ("mkt_2", "grp")))
        clip = jnp.minimum(
            1.0, clip_target / jnp.sqrt(squares / (firm_count * draw_count) + norm_eps)
        )
        owned = owned + clip * gap
        mean_now = mean_now + log_observed - jnp.log(predicted)
    return (mean_now, owned)


def solution(mesh):
    torus = Mesh(
        mesh.devices.reshape(4, 4, 2, mesh.shape["grp"]), ("mkt_0", "mkt_1", "mkt_2", "grp")
    )
    in_specs = (
        P(MKT_GRP, None),
        P(MKT_GRP, None),
        P(MKT_GRP, None, None),
        P(MKT_GRP, None, None),
        P(),
        P(MKT_GRP, None),
        P(MKT_GRP),
        P(MKT_GRP, None),
        P(),
        P(MKT_GRP, None),
        P(),
    )
    out_specs = (P(MKT_GRP, None), P(MKT_GRP, None))
    return jax.shard_map(local, mesh=torus, in_specs=in_specs, out_specs=out_specs, check_vma=False)
```

profile of v0, /device:TPU:1, one launch (start us, length us, event | category | flops | bytes accessed | tf_op | source)
XLA Modules:
  0.0 411.3 jit_solution(3979237312355868021)
XLA Ops:
  1.6 15.7 %all_to_all.93 = f32[16,4,1024]{2,1,0:T(4,128)S(1)} all-to-all(f32[16,4,1024]{2,1,0:T(4,128)S(1)} %broadcast_in_dim.94), channel_id=1, replica_groups=mesh['mkt_0'=4,'mkt_1'=4,'mkt_2'=2,'grp'=4] {'mkt_0','mkt_1'}, dimensions={0} | all-to-all | bytes 524288 | tf_op jit(solution)/shard_map/all_to_all | solution.py:18
  19.1 6.5 %all-to-all-start.1 = ((f32[8,16,4,1024]{3,2,1,0:T(4,128)}), f32[8,16,4,1024]{3,2,1,0:T(4,128)}, u32[]{:S(2)}, u32[]{:S(2)}) async-start(f32[8,16,4,1024]{3,2,1,0:T(4,128)} %broadcast_in_dim.95), calls=%async_computation.1 | async-start | bytes 4194304 | tf_op jit(solution)/shard_map/all_to_all | solution.py:18
  25.6 2.4 scatter_custom_fusion
  28.1 6.9 %gather_fusion = s32[1024]{0:T(1024)S(1)} fusion(s32[512]{0:T(512)S(1)} %scatter_custom_fusion, s32[1024]{0:T(1024)S(1)} %broadcast_clamp_fusion.1), kind=kCustom, calls=%fused_computation.3 | custom fusion | bytes 12288 | tf_op jit(solution)/shard_map/jit(_take)/gather | solution.py:102
  35.3 16.5 %all-to-all-done.1 = f32[8,16,4,1024]{3,2,1,0:T(4,128)} async-done(((f32[8,16,4,1024]{3,2,1,0:T(4,128)}), f32[8,16,4,1024]{3,2,1,0:T(4,128)}, u32[]{:S(2)}, u32[]{:S(2)}) %all-to-all-start.1) | async-done | bytes 2097184 | tf_op jit(solution)/shard_map/all_to_all | solution.py:18
  51.9 3.1 copy.35
  55.0 3.0 reshape_reshape.9
  58.0 8.1 %gather_fusion.2 = f32[1024,1024]{1,0:T(8,128)} fusion(f32[512,1024]{1,0:T(8,128)} %reshape_reshape.9, s32[1024]{0:T(1024)S(1)} %broadcast_clamp_fusion), kind=kCustom, calls=%fused_computation.clone | custom fusion | bytes 8392704 | tf_op jit(solution)/shard_map/jit(_take)/gather | solution.py:66
  66.1 8.2 %fusion.40 = (f32[16,1024]{1,0:T(8,128)S(1)}, f32[16,64,1024]{2,1,0:T(8,128)}, f32[16,64,1024]{2,1,0:T(8,128)}) fusion(f32[16,64,1024]{2,1,0:T(8,128)} %bitcast.33, pred[16,64]{1,0:T(8,128)(4,1)S(1)} %get-tuple-element.19, f32[16,64]{1,0:T(8,128)S(1)} %copy-done.9, f32[16,5,1024]{2,0,1:T(8,128)S(1)} %copy-done.4, f32[16,64,5]{1,0,2:T(8,128)S(1)} %broadcast_multiply_fusion.4), kind=kOutput, calls=%fused_computation.76 | convolution fusion | flops 67092480 | bytes 13001728 | tf_op jit(solution)/shard_map/mjk,mkr->mjr/dot_general | solution.py:107
  75.0 3.5 all-to-all-start.3
  78.6 5.2 %broadcast_multiply_fusion.2 = f32[16,64,1024]{2,1,0:T(8,128)} fusion(f32[16,1024]{1,0:T(8,128)S(1)} %get-tuple-element.16, f32[16,64,1024]{2,1,0:T(8,128)} %get-tuple-element.18, f32[16,1024]{1,0:T(8,128)S(1)} %get-tuple-element.23), kind=kLoop, calls=%fused_computation.22 | loop fusion | flops 2097152 | bytes 8519680 | tf_op jit(solution)/shard_map/mul | solution.py:71
  84.4 3.5 all-to-all-start.4
  87.9 6.2 %fusion.12 = f32[128,1,1,4,1024]{4,0,3,2,1:T(8,128)S(1)} fusion(f32[1024,1024,1]{1,0,2:T(8,128)} %bitcast.36, s32[1024]{0:T(1024)S(1)} %select_n.43, s32[128,4]{0,1:T(4,128)S(1)} %multiply_add_fusion.3), kind=kOutput, calls=%fused_computation.27 | convolution fusion | flops 6442975232 | bytes 6297600 | tf_op jit(solution)/shard_map/dot_general | solution.py:76
  94.0 2.7 copy.36
  96.8 10.2 %all-to-all-start.2 = ((f32[128,1,1,4,1024]{4,3,2,1,0:T(4,128)}), f32[128,1,1,4,1024]{4,3,2,1,0:T(4,128)}, u32[]{:S(2)}, u32[]{:S(2)}) async-start(f32[128,1,1,4,1024]{4,3,2,1,0:T(4,128)} %copy.36), calls=%async_computation.2 | async-start | bytes 4194304 | tf_op jit(solution)/shard_map/all_to_all | solution.py:55
  107.8 29.9 %all-to-all-done.2 = f32[128,1,1,4,1024]{4,3,2,1,0:T(4,128)} async-done(((f32[128,1,1,4,1024]{4,3,2,1,0:T(4,128)}), f32[128,1,1,4,1024]{4,3,2,1,0:T(4,128)}, u32[]{:S(2)}, u32[]{:S(2)}) %all-to-all-start.2) | async-done | bytes 2097184 | tf_op jit(solution)/shard_map/all_to_all | solution.py:55
  137.7 1.9 reduce_sum.173
  140.9 7.5 %all_to_all.94 = f32[8,1,1]{2,1,0:T(1,128)S(1)} all-to-all(f32[8,1,1]{2,1,0:T(1,128)S(1)} %broadcast_in_dim.104), channel_id=1, replica_groups=mesh['mkt_0'=4,'mkt_1'=4,'mkt_2'=2,'grp'=4] {'mkt_2','grp'}, dimensions={0} | all-to-all | bytes 64 | tf_op jit(solution)/shard_map/all_to_all | solution.py:18
  149.7 9.3 %all_to_all.95 = f32[16,1,1]{2,1,0:T(1,128)S(1)} all-to-all(f32[16,1,1]{2,1,0:T(1,128)S(1)} %broadcast_in_dim.105), channel_id=1, replica_groups=mesh['mkt_0'=4,'mkt_1'=4,'mkt_2'=2,'grp'=4] {'mkt_0','mkt_1'}, dimensions={0} | all-to-all | bytes 128 | tf_op jit(solution)/shard_map/all_to_all | solution.py:18
  160.4 10.1 %all_to_all.96 = f32[16,4,1024]{2,1,0:T(4,128)S(1)} all-to-all(f32[16,4,1024]{2,1,0:T(4,128)S(1)} %broadcast_in_dim.106), channel_id=1, replica_groups=mesh['mkt_0'=4,'mkt_1'=4,'mkt_2'=2,'grp'=4] {'mkt_0','mkt_1'}, dimensions={0} | all-to-all | bytes 524288 | tf_op jit(solution)/shard_map/all_to_all | solution.py:18
  170.5 1.9 broadcast_in_dim.107
  172.4 7.0 %all-to-all-start.8 = ((f32[8,16,4,1024]{3,2,1,0:T(4,128)}), f32[8,16,4,1024]{3,2,1,0:T(4,128)S(1)}, u32[]{:S(2)}, u32[]{:S(2)}) async-start(f32[8,16,4,1024]{3,2,1,0:T(4,128)} %broadcast_in_dim.107), calls=%async_computation.8 | async-start | bytes 4194304 | tf_op jit(solution)/shard_map/all_to_all | solution.py:18
  179.4 5.5 %fusion.9 = f32[16,1,64]{2,1,0:T(1,128)S(1)} fusion(f32[16,64,1024]{2,1,0:T(8,128)} %get-tuple-element.18, f32[16,1024]{1,0:T(8,128)S(1)} %get-tuple-element.23, f32[16,1024,1]{1,0,2:T(8,128)S(1)} %bitcast.39), kind=kOutput, calls=%fused_computation.24 | convolution fusion | flops 13631488 | bytes 4329472 | tf_op jit(solution)/shard_map/mjr,mr->mj/dot_general | solution.py:68
  185.0 20.6 %all-to-all-done.8 = f32[8,16,4,1024]{3,2,1,0:T(4,128)S(1)} async-done(((f32[8,16,4,1024]{3,2,1,0:T(4,128)}), f32[8,16,4,1024]{3,2,1,0:T(4,128)S(1)}, u32[]{:S(2)}, u32[]{:S(2)}) %all-to-all-start.8) | async-done | bytes 2097184 | tf_op jit(solution)/shard_map/all_to_all | solution.py:18
  207.2 2.0 reshape_reshape.10
  209.2 5.4 %gather_fusion.3 = f32[1024,1024]{1,0:T(8,128)} fusion(f32[512,1024]{1,0:T(8,128)S(1)} %reshape_reshape.10, s32[1024]{0:T(1024)S(1)} %broadcast_clamp_fusion), kind=kCustom, calls=%fused_computation.1.clone | custom fusion | bytes 8392704 | tf_op jit(solution)/shard_map/jit(_take)/gather | solution.py:66
  214.6 4.0 fusion.37
  221.0 3.7 fusion.15
  226.1 35.6 %all_to_all.97 = f32[128,1,1,4,1024]{4,3,2,1,0:T(4,128)} all-to-all(f32[128,1,1,4,1024]{4,3,2,1,0:T(4,128)S(1)} %copy.42), channel_id=1, replica_groups=mesh['mkt_0'=4,'mkt_1'=4,'mkt_2'=2,'grp'=4] {'mkt_0','mkt_1','mkt_2','grp'}, dimensions={0} | all-to-all | bytes 4194304 | tf_op jit(solution)/shard_map/all_to_all | solution.py:55
  261.7 1.9 reduce_sum.181
  265.0 7.5 %all_to_all.98 = f32[8,1,1]{2,1,0:T(1,128)S(1)} all-to-all(f32[8,1,1]{2,1,0:T(1,128)S(1)} %broadcast_in_dim.108), channel_id=1, replica_groups=mesh['mkt_0'=4,'mkt_1'=4,'mkt_2'=2,'grp'=4] {'mkt_2','grp'}, dimensions={0} | all-to-all | bytes 64 | tf_op jit(solution)/shard_map/all_to_all | solution.py:18
  273.7 9.2 %all_to_all.99 = f32[16,1,1]{2,1,0:T(1,128)S(1)} all-to-all(f32[16,1,1]{2,1,0:T(1,128)S(1)} %broadcast_in_dim.109), channel_id=1, replica_groups=mesh['mkt_0'=4,'mkt_1'=4,'mkt_2'=2,'grp'=4] {'mkt_0','mkt_1'}, dimensions={0} | all-to-all | bytes 128 | tf_op jit(solution)/shard_map/all_to_all | solution.py:18
  284.2 10.1 %all_to_all.100 = f32[16,4,1024]{2,1,0:T(4,128)S(1)} all-to-all(f32[16,4,1024]{2,1,0:T(4,128)S(1)} %broadcast_in_dim.110), channel_id=1, replica_groups=mesh['mkt_0'=4,'mkt_1'=4,'mkt_2'=2,'grp'=4] {'mkt_0','mkt_1'}, dimensions={0} | all-to-all | bytes 524288 | tf_op jit(solution)/shard_map/all_to_all | solution.py:18
  296.3 7.0 %all-to-all-start.13 = ((f32[8,16,4,1024]{3,2,1,0:T(4,128)}), f32[8,16,4,1024]{3,2,1,0:T(4,128)S(1)}, u32[]{:S(2)}, u32[]{:S(2)}) async-start(f32[8,16,4,1024]{3,2,1,0:T(4,128)} %broadcast_in_dim.111), calls=%async_computation.13 | async-start | bytes 4194304 | tf_op jit(solution)/shard_map/all_to_all | solution.py:18
  303.2 5.5 %fusion.10 = f32[16,1,64]{2,1,0:T(1,128)S(1)} fusion(f32[16,64,1024]{2,1,0:T(8,128)} %copy-done.2, f32[16,1024]{1,0:T(8,128)S(1)} %broadcast_add_fusion.1, f32[16,1024,1]{1,0,2:T(8,128)S(1)} %bitcast.40), kind=kOutput, calls=%fused_computation.25 | convolution fusion | flops 13631488 | bytes 4329472 | tf_op jit(solution)/shard_map/mjr,mr->mj/dot_general | solution.py:68
  308.8 20.6 %all-to-all-done.13 = f32[8,16,4,1024]{3,2,1,0:T(4,128)S(1)} async-done(((f32[8,16,4,1024]{3,2,1,0:T(4,128)}), f32[8,16,4,1024]{3,2,1,0:T(4,128)S(1)}, u32[]{:S(2)}, u32[]{:S(2)}) %all-to-all-start.13) | async-done | bytes 2097184 | tf_op jit(solution)/shard_map/all_to_all | solution.py:18
  331.0 2.0 reshape_reshape.11
  333.0 5.4 %gather_fusion.4 = f32[1024,1024]{1,0:T(8,128)} fusion(f32[512,1024]{1,0:T(8,128)S(1)} %reshape_reshape.11, s32[1024]{0:T(1024)S(1)} %broadcast_clamp_fusion), kind=kCustom, calls=%fused_computation.2.clone | custom fusion | bytes 8392704 | tf_op jit(solution)/shard_map/jit(_take)/gather | solution.py:66
  338.4 4.0 fusion.35
  344.8 3.7 fusion.18
  348.5 2.7 copy.46
  351.2 5.2 %all-to-all-start.14 = ((f32[128,1,1,4,1024]{4,3,2,1,0:T(4,128)}), f32[128,1,1,4,1024]{4,3,2,1,0:T(4,128)}, u32[]{:S(2)}, u32[]{:S(2)}) async-start(f32[128,1,1,4,1024]{4,3,2,1,0:T(4,128)} %copy.46), calls=%async_computation.14 | async-start | bytes 4194304 | tf_op jit(solution)/shard_map/all_to_all | solution.py:55
  356.4 5.7 %fusion.11 = f32[16,1,64]{2,1,0:T(1,128)S(1)} fusion(f32[16,64,1024]{2,1,0:T(8,128)} %copy-done.3, f32[16,1024]{1,0:T(8,128)S(1)} %broadcast_add_fusion, f32[16,1024,1]{1,0,2:T(8,128)S(1)} %bitcast.41), kind=kOutput, calls=%fused_computation.26 | convolution fusion | flops 13631488 | bytes 4329472 | tf_op jit(solution)/shard_map/mjr,mr->mj/dot_general | solution.py:68
  362.1 24.9 %all-to-all-done.14 = f32[128,1,1,4,1024]{4,3,2,1,0:T(4,128)} async-done(((f32[128,1,1,4,1024]{4,3,2,1,0:T(4,128)}), f32[128,1,1,4,1024]{4,3,2,1,0:T(4,128)}, u32[]{:S(2)}, u32[]{:S(2)}) %all-to-all-start.14) | async-done | bytes 2097184 | tf_op jit(solution)/shard_map/all_to_all | solution.py:55
  387.0 1.9 reduce_sum.186
  390.3 7.5 %all_to_all.101 = f32[8,1,1]{2,1,0:T(1,128)S(1)} all-to-all(f32[8,1,1]{2,1,0:T(1,128)S(1)} %broadcast_in_dim.112), channel_id=1, replica_groups=mesh['mkt_0'=4,'mkt_1'=4,'mkt_2'=2,'grp'=4] {'mkt_2','grp'}, dimensions={0} | all-to-all | bytes 64 | tf_op jit(solution)/shard_map/all_to_all | solution.py:18
  399.6 3.5 all-to-all-start.16
  403.8 5.6 %all-to-all-done.16 = f32[16,1,1]{2,1,0:T(1,128)S(1)} async-done(((f32[16,1,1]{2,1,0:T(1,128)}), f32[16,1,1]{2,1,0:T(1,128)S(1)}, u32[]{:S(2)}, u32[]{:S(2)}) %all-to-all-start.16) | async-done | bytes 96 | tf_op jit(solution)/shard_map/all_to_all | solution.py:18
  (84 shorter events, 28.1 us)
Async XLA Ops:
  0.6 106.5 %copy-start = (f32[512,1024]{1,0:T(8,128)S(1)}, f32[512,1024]{1,0:T(8,128)}, u32[]{:S(2)}) copy-start(f32[512,1024]{1,0:T(8,128)} %param.23) | copy-start | bytes 6291460
  0.6 24.9 %copy-start.10 = (s32[16,64]{1,0:T(8,128)S(1)}, s32[16,64]{1,0:T(8,128)}, u32[]{:S(2)}) copy-start(s32[16,64]{1,0:T(8,128)} %param.20) | copy-start | bytes 12292
  0.7 25.0 %copy-start.11 = (s32[512]{0:T(512)S(1)}, s32[512]{0:T(512)}, u32[]{:S(2)}) copy-start(s32[512]{0:T(512)} %param.21) | copy-start | bytes 6148
  19.1 32.8 %all-to-all-start.1 = ((f32[8,16,4,1024]{3,2,1,0:T(4,128)}), f32[8,16,4,1024]{3,2,1,0:T(4,128)}, u32[]{:S(2)}, u32[]{:S(2)}) async-start(f32[8,16,4,1024]{3,2,1,0:T(4,128)} %broadcast_in_dim.95), calls=%async_computation.1 | async-start | bytes 4194304 | tf_op jit(solution)/shard_map/all_to_all | solution.py:18
  28.1 7.1 %copy-start.8 = (f32[16,64,5]{1,0,2:T(8,128)S(1)}, f32[16,64,5]{1,0,2:T(8,128)}, u32[]{:S(2)}) copy-start(f32[16,64,5]{1,0,2:T(8,128)} %param.15) | copy-start | bytes 61444
  28.1 7.1 %copy-start.12 = (f32[5]{0:T(128)S(1)}, f32[5]{0:T(128)}, u32[]{:S(2)}) copy-start(f32[5]{0:T(128)} %param.17) | copy-start | bytes 64
  58.0 8.1 %copy-start.4 = (f32[16,5,1024]{2,0,1:T(8,128)S(1)}, f32[16,5,1024]{2,0,1:T(8,128)}, u32[]{:S(2)}) copy-start(f32[16,5,1024]{2,0,1:T(8,128)} %param.16) | copy-start | bytes 983044
  58.0 8.1 %copy-start.9 = (f32[16,64]{1,0:T(8,128)S(1)}, f32[16,64]{1,0:T(8,128)}, u32[]{:S(2)}) copy-start(f32[16,64]{1,0:T(8,128)} %param.13) | copy-start | bytes 12292
  66.1 8.2 %copy-start.7 = (f32[16,1024]{1,0:T(8,128)S(1)}, f32[16,1024]{1,0:T(8,128)}, u32[]{:S(2)}) copy-start(f32[16,1024]{1,0:T(8,128)} %param.18) | copy-start | bytes 196612
  66.1 8.2 %copy-start.13 = (f32[16]{0:T(128)S(1)}, f32[16]{0:T(128)}, u32[]{:S(2)}) copy-start(f32[16]{0:T(128)} %param.19) | copy-start | bytes 196
  75.0 8.7 %all-to-all-start.3 = ((f32[8,1,1024]{2,1,0:T(1,128)}), f32[8,1,1024]{2,1,0:T(1,128)S(1)}, u32[]{:S(2)}, u32[]{:S(2)}) async-start(f32[8,1,1024]{2,1,0:T(1,128)} %broadcast_in_dim.102), calls=%async_computation.3 | async-start | bytes 65536 | tf_op jit(solution)/shard_map/all_to_all | solution.py:18
  84.4 12.4 %all-to-all-start.4 = ((f32[16,1,1024]{2,1,0:T(1,128)}), f32[16,1,1024]{2,1,0:T(1,128)S(1)}, u32[]{:S(2)}, u32[]{:S(2)}) async-start(f32[16,1,1024]{2,1,0:T(1,128)} %broadcast_in_dim.103), calls=%async_computation.4 | async-start | bytes 131072 | tf_op jit(solution)/shard_map/all_to_all | solution.py:18
  96.8 63.5 %copy-start.6 = (f32[4,1024]{1,0:T(4,128)S(1)}, f32[4,1024]{1,0:T(4,128)}, u32[]{:S(2)}) copy-start(f32[4,1024]{1,0:T(4,128)} %param.22) | copy-start | bytes 49156
  96.8 40.9 %all-to-all-start.2 = ((f32[128,1,1,4,1024]{4,3,2,1,0:T(4,128)}), f32[128,1,1,4,1024]{4,3,2,1,0:T(4,128)}, u32[]{:S(2)}, u32[]{:S(2)}) async-start(f32[128,1,1,4,1024]{4,3,2,1,0:T(4,128)} %copy.36), calls=%async_computation.2 | async-start | bytes 4194304 | tf_op jit(solution)/shard_map/all_to_all | solution.py:55
  172.4 33.2 %all-to-all-start.8 = ((f32[8,16,4,1024]{3,2,1,0:T(4,128)}), f32[8,16,4,1024]{3,2,1,0:T(4,128)S(1)}, u32[]{:S(2)}, u32[]{:S(2)}) async-start(f32[8,16,4,1024]{3,2,1,0:T(4,128)} %broadcast_in_dim.107), calls=%async_computation.8 | async-start | bytes 4194304 | tf_op jit(solution)/shard_map/all_to_all | solution.py:18
  179.4 5.5 %copy-start.5 = (f32[16,64]{1,0:T(8,128)S(1)}, f32[16,64]{1,0:T(8,128)}, u32[]{:S(2)}) copy-start(f32[16,64]{1,0:T(8,128)} %param.14) | copy-start | bytes 12292
  218.7 2.3 copy-start.2
  296.3 33.2 %all-to-all-start.13 = ((f32[8,16,4,1024]{3,2,1,0:T(4,128)}), f32[8,16,4,1024]{3,2,1,0:T(4,128)S(1)}, u32[]{:S(2)}, u32[]{:S(2)}) async-start(f32[8,16,4,1024]{3,2,1,0:T(4,128)} %broadcast_in_dim.111), calls=%async_computation.13 | async-start | bytes 4194304 | tf_op jit(solution)/shard_map/all_to_all | solution.py:18
  342.5 2.3 copy-start.3
  351.2 35.8 %all-to-all-start.14 = ((f32[128,1,1,4,1024]{4,3,2,1,0:T(4,128)}), f32[128,1,1,4,1024]{4,3,2,1,0:T(4,128)}, u32[]{:S(2)}, u32[]{:S(2)}) async-start(f32[128,1,1,4,1024]{4,3,2,1,0:T(4,128)} %copy.46), calls=%async_computation.14 | async-start | bytes 4194304 | tf_op jit(solution)/shard_map/all_to_all | solution.py:55
  356.4 54.9 %copy-start.1 = (f32[512,1024]{1,0:T(8,128)S(1)}, f32[512,1024]{1,0:T(8,128)}, u32[]{:S(2)}) copy-start(f32[512,1024]{1,0:T(8,128)} %param.23) | copy-start | bytes 6291460
  399.6 9.8 %all-to-all-start.16 = ((f32[16,1,1]{2,1,0:T(1,128)}), f32[16,1,1]{2,1,0:T(1,128)S(1)}, u32[]{:S(2)}, u32[]{:S(2)}) async-start(f32[16,1,1]{2,1,0:T(1,128)} %broadcast_in_dim.113), calls=%async_computation.16 | async-start | bytes 16384 | tf_op jit(solution)/shard_map/all_to_all | solution.py:18
where the time goes:
time: 413 us; the launch traced here: 411 us
  waiting for transfers between devices  118 us (29%)
  blocking collectives  112 us (27%)
  local copies, waits for them, and re-layouts  64.2 us (16%)
  starting transfers between devices  46.4 us (11%)
  matrix products  38.5 us (9%)
  other arithmetic  28.7 us (7%)
    all_to_all x8, blocking collectives, sent_to_all(): return lax.all_to_all(copies, axis, split_axis=0, concat_axis=0, tiled=True)  76.8 us
    all_to_all x6, waiting for transfers between devices, sent_to_all(): return lax.all_to_all(copies, axis, split_axis=0, concat_axis=0, tiled=True)  63.4 us
    all_to_all x2, waiting for transfers between devices, one_exchange(): tiles = lax.all_to_all(tiles, axis, split_axis=0, concat_axis=0, tiled=True)  54.8 us
    all_to_all x1, blocking collectives, one_exchange(): tiles = lax.all_to_all(tiles, axis, split_axis=0, concat_axis=0, tiled=True)  35.6 us
    all_to_all x6, starting transfers between devices, sent_to_all(): return lax.all_to_all(copies, axis, split_axis=0, concat_axis=0, tiled=True)  30.9 us
    gather x3, local copies, waits for them, and re-layouts, market_terms(): jnp.take(table, row_ids, axis=0)  19 us
    dot_general x3, matrix products, market_terms(): jnp.einsum('mjr,mr->mj', choice_prob, type_weight, precision=lax.Precisio...  16.7 us
    all_to_all x2, starting transfers between devices, one_exchange(): tiles = lax.all_to_all(tiles, axis, split_axis=0, concat_axis=0, tiled=True)  15.4 us
  transfers between devices with their start and end apart: 8, of which 6 were waited for; matrix products, arithmetic and copies ran while one was open for 10% of the time, Pallas kernels for 0%

commit v1 on v0

v1 whole, which is shorter than its diff:
```python
import functools

import jax
import jax.numpy as jnp
from jax import lax
from jax.experimental import pallas as pl
from jax.experimental.pallas import tpu as pltpu
from jax.sharding import Mesh
from jax.sharding import PartitionSpec as P

ITERS = 3
CLIP_TARGET = 0.5
NORM_EPS = 1e-06
AXES = ("mkt_0", "mkt_1", "mkt_2", "grp")
MESH = pl.DeviceIdType.MESH
F32 = jnp.float32
BF16 = jnp.bfloat16


def split_hi_lo(value):
    hi = value.astype(BF16)
    lo = (value - hi.astype(F32)).astype(BF16)
    return hi, lo


def kernel(
    dims,
    pk_ref,
    share_ref,
    size_ref,
    weight_ref,
    loy_ref,
    order_ref,
    order_row_ref,
    draws_hbm,
    fshare_hbm,
    mean_out,
    loy_out,
    pk,
    mass_loc,
    mass,
    draws_loc,
    draws,
    fshare,
    fs_own,
    order_col,
    loy_in,
    own_table,
    table,
    tmass_s,
    tmass_r,
    onehot,
    onehot_t,
    util,
    gath,
    weighted,
    terms,
    acc,
    part,
    rs,
    pred,
    pred_r,
    dmean,
    dmean_s,
    gap_s,
    ag,
    sq_s,
    sq_r,
    sq2_s,
    sq2_r,
    loy_s,
    loc_sem,
    send,
    recv,
):
    nx, nz, nc, ny, mdev, ntraits, firms, draws_all, own = dims
    nh = nc * ny
    ng = nx * nz
    rows = firms // ng
    mrows = mdev * 64
    x, z, c, y = (lax.axis_index(a) for a in AXES)
    g = x * nz + z
    h = c * ny + y
    hpeers = [(dc, dy) for dc in range(nc) for dy in range(ny) if (dc, dy) != (0, 0)]
    gpeers = [(dx, dz) for dx in range(nx) for dz in range(nz) if (dx, dz) != (0, 0)]

    def hdev(dc, dy):
        return lax.rem(c + dc, nc), lax.rem(y + dy, ny)

    def gdev(dx, dz):
        return lax.rem(x + dx, nx), lax.rem(z + dz, nz)

    def lanes(index):
        return pl.ds(pl.multiple_of(index * 128, 128), 128)

    started = []

    def push(stage, src, dst, device):
        copy = pltpu.make_async_remote_copy(
            src_ref=src,
            dst_ref=dst,
            send_sem=send.at[stage],
            recv_sem=recv.at[stage],
            device_id=device,
            device_id_type=MESH,
        )
        copy.start()

    def to_h(stage, src_of, dst):
        for dc, dy in hpeers:
            c2, y2 = hdev(dc, dy)
            push(stage, src_of(c2 * ny + y2), dst, (x, z, c2, y2))

    def to_g(stage, src_of, dst_of):
        for dx, dz in gpeers:
            x2, z2 = gdev(dx, dz)
            push(stage, src_of(x2 * nz + z2), dst_of(dx * nz + dz), (x2, z2, c, y))

    def arrived(stage, like):
        started.append((stage, like))
        pltpu.make_async_copy(like, like, recv.at[stage]).wait()

    local = []

    def keep(src, dst):
        copy = pltpu.make_async_copy(src, dst, loc_sem.at[len(local)])
        copy.start()
        local.append(copy)
        return copy

    get_draws = keep(draws_hbm, draws_loc)
    get_share = keep(fshare_hbm.at[:, lanes(h)], fshare)

    barrier = pltpu.get_barrier_semaphore()
    for dc, dy in hpeers:
        c2, y2 = hdev(dc, dy)
        pl.semaphore_signal(barrier, inc=1, device_id=(x, z, c2, y2), device_id_type=MESH)
    for dx, dz in gpeers:
        x2, z2 = gdev(dx, dz)
        pl.semaphore_signal(barrier, inc=1, device_id=(x2, z2, c, y), device_id_type=MESH)

    mass_all = weight_ref[...] * size_ref[...]
    mass_loc[...] = mass_all
    row_mass = jnp.sum(mass_all, axis=1, keepdims=True)
    lane_market = lax.broadcasted_iota(jnp.int32, (mdev, 128), 1) // 8
    market = lax.broadcasted_iota(jnp.int32, (mdev, 128), 0)
    denom = jnp.sum(jnp.where(lane_market == market, row_mass, 0.0), axis=0, keepdims=True)
    for b in range(firms // 128):
        row = order_row_ref[:, b * 128 : (b + 1) * 128]
        order_col[b * 128 : (b + 1) * 128, :] = jnp.broadcast_to(row, (128, 128)).T

    pl.semaphore_wait(barrier, len(hpeers) + len(gpeers))

    to_h(0, lambda h2: pk_ref, pk.at[h])
    keep_pk = keep(pk_ref, pk.at[h])
    to_h(1, lambda h2: loy_ref.at[:, lanes(h2)], loy_in.at[h])
    keep_loy = keep(loy_ref.at[:, lanes(h)], loy_in.at[h])
    to_h(2, lambda h2: mass_loc.at[:, lanes(h2)], mass.at[h])
    keep_mass = keep(mass_loc.at[:, lanes(h)], mass.at[h])
    get_draws.wait()
    to_h(3, lambda h2: draws_loc.at[:, :, lanes(h2)], draws.at[h])
    keep_draws = keep(draws_loc.at[:, :, lanes(h)], draws.at[h])

    get_share.wait()
    for k in range(rows):
        fs_own[k : k + 1, :] = fshare[pl.ds(order_ref[g * rows + k], 1), :]
    fs_own[...] = jnp.log(fs_own[...])

    keep_pk.wait()
    arrived(0, pk.at[pl.ds(0, nh - 1)])

    def build(hh, carry):
        ids = pk[hh, ntraits + 1]
        ids_rows = pk[hh, ntraits + 2]
        order_row = order_row_ref[...]
        for b in range(mrows // 16):
            col = jnp.concatenate([ids[:, 2 * b : 2 * b + 1], ids[:, 2 * b + 1 : 2 * b + 2]], axis=0)
            hot = jnp.where(col == order_row, 1.0, 0.0).astype(BF16)
            onehot[pl.ds(pl.multiple_of(hh * mrows + b * 16, 16), 16), :] = hot
        for p in range(mrows // 128):
            row = ids_rows[p : p + 1, :]
            hot = jnp.where(order_col[...] == row, 1.0, 0.0).astype(BF16)
            onehot_t[hh, :, p * 128 : (p + 1) * 128] = hot
        return carry

    lax.fori_loop(0, nh, build, 0)

    keep_loy.wait()
    arrived(1, loy_in.at[pl.ds(0, nh - 1)])
    for hh in range(nh):
        own_table[hh * own : (hh + 1) * own, :] = loy_in[hh]
    to_g(4, lambda g2: own_table, lambda slot: table.at[g])
    keep_own = keep(own_table, table.at[g])

    keep_mass.wait()
    arrived(2, mass.at[pl.ds(0, nh - 1)])
    tm = jnp.sum(mass[...].reshape(nh * mdev, 128), axis=0, keepdims=True)
    tmass_s[...] = jnp.broadcast_to(tm, (8, 128))
    to_g(5, lambda g2: tmass_s, lambda slot: tmass_r.at[slot])

    keep_own.wait()
    arrived(4, table.at[pl.ds(0, ng - 1)])
    keep_draws.wait()
    arrived(3, draws.at[pl.ds(0, nh - 1)])

    lane = lax.broadcasted_iota(jnp.int32, (8, 128), 1)
    mean_now = pk_ref[0]
    log_share = jnp.log(share_ref[...])
    type_mass = None
    clip = None

    for step in range(ITERS):
        source = table if step == 0 else ag.at[step - 1]
        hi, lo = split_hi_lo(source[...].reshape(firms, 128))
        terms[:, :128] = hi
        terms[:, 128:] = lo

        def market_block(hh, carry, step=step, clip=clip):
            base = pl.multiple_of(hh * mrows, mrows)
            gath[...] = jnp.dot(
                onehot[pl.ds(base, mrows), :], terms[...], preferred_element_type=F32
            )
            compact = jnp.zeros((8, 128), F32)
            if step == 0:
                cols = [pk[hh, k] for k in range(ntraits + 1)]
            else:
                cols = [dmean[step - 1, hh]]
            for m in range(mdev):
                expu = []
                total = None
                if step == 0:
                    shocks = draws[hh, m]
                for jb in range(8):
                    at = m * 64 + jb * 8
                    lane_at = m * 8 + jb
                    moved = gath[at : at + 8, :128] + gath[at : at + 8, 128:]
                    where = pl.ds(pl.multiple_of(base + at, 8), 8)
                    if step == 0:
                        u = moved + cols[0][:, lane_at : lane_at + 1]
                        for k in range(ntraits):
                            u = u + cols[k + 1][:, lane_at : lane_at + 1] * shocks[k : k + 1, :]
                    else:
                        u = util[where, :] + (clip * moved + cols[0][:, lane_at : lane_at + 1])
                    if step < ITERS - 1:
                        util[where, :] = u
                    e = jnp.exp(u)
                    expu.append(e)
                    total = e if total is None else total + e
                total = jnp.sum(total, axis=0, keepdims=True)
                scale = mass[hh, m : m + 1, :] / (1.0 + total)
                wts = []
                for jb in range(8):
                    wt = expu[jb] * scale
                    wts.append(wt)
                    red = jnp.sum(wt, axis=1, keepdims=True)
                    compact = jnp.where(lane == m * 8 + jb, red, compact)
                for jb in range(0, 8, 2):
                    at = m * 64 + jb * 8
                    hi, lo = split_hi_lo(jnp.concatenate([wts[jb], wts[jb + 1]], axis=0))
                    weighted[at : at + 16, :128] = hi
                    weighted[at : at + 16, 128:] = lo
            pred[step, hh] = compact
            new = jnp.dot(onehot_t[hh], weighted[...], preferred_element_type=F32)
            acc[...] = acc[...] + new
            return carry

        acc[...] = jnp.zeros(acc.shape, F32)
        lax.fori_loop(0, nh, market_block, 0)

        base_stage = 6 + 6 * step
        to_h(base_stage, lambda h2: pred.at[step, h2], pred_r.at[step, h])
        part[step] = (acc[:, :128] + acc[:, 128:]).reshape(ng, rows, 128)
        to_g(base_stage + 1, lambda g2: part.at[step, g2], lambda slot: rs.at[step, slot - 1])

        arrived(base_stage, pred_r.at[step, pl.ds(0, nh - 1)])
        pred_r[step, h] = pred[step, h]
        num = jnp.sum(pred_r[step], axis=0)
        delta = log_share - jnp.log(num / denom)
        mean_now = mean_now + delta
        if step < ITERS - 1:
            dmean_s[step] = delta
            dmean[step, h] = delta
            to_h(base_stage + 2, lambda h2: dmean_s.at[step], dmean.at[step, h])

        if step == 0:
            arrived(5, tmass_r.at[pl.ds(1, ng - 1)])
            type_mass = tmass_s[0:1, :]
            for slot in range(1, ng):
                type_mass = type_mass + tmass_r[slot, 0:1, :]
        arrived(base_stage + 1, rs.at[step])
        totals = part[step, g]
        for slot in range(ng - 1):
            totals = totals + rs[step, slot]
        gap = fs_own[...] - jnp.log(totals / type_mass)
        if step < ITERS - 1:
            gap_s[step] = gap
            ag[step, g] = gap
            to_g(base_stage + 3, lambda g2: gap_s.at[step], lambda slot: ag.at[step, g])
        sq = jnp.sum((gap * gap).reshape(rows // 8, 8, 128), axis=0)
        sq_s[step] = sq
        sq_r[step, h] = sq
        to_h(base_stage + 4, lambda h2: sq_s.at[step], sq_r.at[step, h])
        arrived(base_stage + 4, sq_r.at[step, pl.ds(0, nh - 1)])
        sq = jnp.sum(sq_r[step], axis=0)
        sq2_s[step] = sq
        sq2_r[step, 0] = sq
        to_g(base_stage + 5, lambda g2: sq2_s.at[step], lambda slot: sq2_r.at[step, slot])
        arrived(base_stage + 5, sq2_r.at[step, pl.ds(1, ng - 1)])
        sq = jnp.sum(jnp.sum(sq2_r[step], axis=0), axis=0, keepdims=True)
        sq = jnp.sum(sq, axis=1, keepdims=True)
        clip = jnp.minimum(
            1.0, CLIP_TARGET / jnp.sqrt(sq / (firms * draws_all) + NORM_EPS)
        )
        own_new = (own_table[...] if step == 0 else own_new) + clip * gap
        if step < ITERS - 1:
            arrived(base_stage + 3, ag.at[step, pl.ds(0, ng - 1)])
            arrived(base_stage + 2, dmean.at[step, pl.ds(0, nh - 1)])

    mean_out[...] = mean_now
    for hh in range(nh):
        loy_s[hh] = own_new[hh * own : (hh + 1) * own, :]
    last = 6 + 6 * ITERS
    to_h(last, lambda h2: loy_s.at[h2], loy_out.at[:, lanes(h)])
    keep_out = keep(loy_s.at[h], loy_out.at[:, lanes(h)])
    keep_out.wait()
    arrived(last, loy_out.at[:, pl.ds(0, 128 * (nh - 1))])
    for stage, like in started:
        pltpu.make_async_copy(like, like, send.at[stage]).wait()


def local(
    mean_utility,
    market_share,
    product_traits,
    taste_draws,
    taste_scale,
    type_weight,
    market_size,
    product_firm,
    firm_order,
    loyalty,
    firm_share,
    shape,
):
    nx, nz, nc, ny = shape
    nh, ng = nc * ny, nx * nz
    mdev, ntraits, draws_all = taste_draws.shape
    firms = firm_share.shape[0]
    own = loyalty.shape[0]
    rows = firms // ng

    def columns(array):
        return array.reshape(mdev, 8, 8).transpose(2, 0, 1).reshape(8, 128)

    ids = product_firm.astype(F32)
    traits = (product_traits * taste_scale).reshape(mdev, 8, 8, ntraits)
    traits = traits.transpose(3, 2, 0, 1).reshape(ntraits, 8, 128)
    pk = jnp.concatenate(
        [columns(mean_utility)[None], traits, columns(ids)[None], ids.reshape(1, 8, 128)], axis=0
    )
    kinds = pk.shape[0]
    dims = (nx, nz, nc, ny, mdev, ntraits, firms, draws_all, own)
    vmem = pl.BlockSpec(memory_space=pltpu.VMEM)
    anywhere = pl.BlockSpec(memory_space=pl.ANY)
    scratch = [
        ((nh, kinds, 8, 128), F32),
        ((mdev, draws_all), F32),
        ((nh, mdev, 128), F32),
        ((mdev, ntraits, draws_all), F32),
        ((nh, mdev, ntraits, 128), F32),
        ((firms, 128), F32),
        ((rows, 128), F32),
        ((firms, 128), F32),
        ((nh, own, 128), F32),
        ((rows, 128), F32),
        ((ng, rows, 128), F32),
        ((8, 128), F32),
        ((ng, 8, 128), F32),
        ((nh * mdev * 64, firms), BF16),
        ((nh, firms, mdev * 64), BF16),
        ((nh * mdev * 64, 128), F32),
        ((mdev * 64, 256), F32),
        ((mdev * 64, 256), BF16),
        ((firms, 256), BF16),
        ((firms, 256), F32),
        ((ITERS, ng, rows, 128), F32),
        ((ITERS, ng - 1, rows, 128), F32),
        ((ITERS, nh, 8, 128), F32),
        ((ITERS, nh, 8, 128), F32),
        ((ITERS - 1, nh, 8, 128), F32),
        ((ITERS - 1, 8, 128), F32),
        ((ITERS - 1, rows, 128), F32),
        ((ITERS - 1, ng, rows, 128), F32),
        ((ITERS, 8, 128), F32),
        ((ITERS, nh, 8, 128), F32),
        ((ITERS, 8, 128), F32),
        ((ITERS, ng, 8, 128), F32),
        ((nh, own, 128), F32),
    ]
    stages = 6 + 6 * ITERS + 1
    mean, loy = pl.pallas_call(
        functools.partial(kernel, dims),
        name="contraction",
        out_shape=(
            jax.ShapeDtypeStruct((8, 128), F32),
            jax.ShapeDtypeStruct((own, draws_all), F32),
        ),
        in_specs=[vmem, vmem, vmem, vmem, vmem, pl.BlockSpec(memory_space=pltpu.SMEM), vmem]
        + [anywhere, anywhere],
        out_specs=(vmem, vmem),
        scratch_shapes=[pltpu.VMEM(s, d) for s, d in scratch]
        + [
            pltpu.SemaphoreType.DMA((8,)),
            pltpu.SemaphoreType.DMA((stages,)),
            pltpu.SemaphoreType.DMA((stages,)),
        ],
        compiler_params=pltpu.CompilerParams(
            collective_id=0, has_side_effects=True, vmem_limit_bytes=60 * 1024 * 1024
        ),
    )(
        pk,
        columns(market_share),
        market_size.reshape(mdev, 1),
        type_weight,
        loyalty,
        firm_order,
        firm_order.astype(F32).reshape(1, firms),
        taste_draws,
        firm_share,
    )
    mean = mean.reshape(8, mdev, 8).transpose(1, 2, 0).reshape(mdev, 64)
    return mean, loy


def solution(mesh):
    shape = (4, 4, 2, mesh.shape["grp"])
    torus = Mesh(mesh.devices.reshape(shape), AXES)
    in_specs = (
        P(AXES, None),
        P(AXES, None),
        P(AXES, None, None),
        P(AXES, None, None),
        P(),
        P(AXES, None),
        P(AXES),
        P(AXES, None),
        P(),
        P(AXES, None),
        P(),
    )
    out_specs = (P(AXES, None), P(AXES, None))
    return jax.shard_map(
        functools.partial(local, shape=shape),
        mesh=torus,
        in_specs=in_specs,
        out_specs=out_specs,
        check_vma=False,
    )
```

time: 413 us -> 130 us (0.31)
  waiting for transfers between devices: 118 us -> 0 us
  Pallas kernels: 0 us -> 116 us
  blocking collectives: 112 us -> 0 us
  local copies, waits for them, and re-layouts: 64.2 us -> 9.24 us
  starting transfers between devices: 46.4 us -> 0 us
  matrix products: 38.5 us -> 0 us
  other arithmetic: 28.7 us -> 3.36 us
    all_to_all x8 -> x0, waiting for transfers between devices: 118 us -> none  [the longest x6 63.4 us: sent_to_all(): return lax.all_to_all(copies, axis, split_axis=0, concat_axis=0, tiled=True)]
    pallas_call x0 -> x1, Pallas kernels: none -> 116 us  [local(): pl.pallas_call(functools.partial(kernel, dims), name='contraction', out_s...]
    all_to_all x9 -> x0, blocking collectives: 112 us -> none  [the longest x8 76.8 us: sent_to_all(): return lax.all_to_all(copies, axis, split_axis=0, concat_axis=0, tiled=True)]
    all_to_all x8 -> x0, starting transfers between devices: 46.4 us -> none  [the longest x6 30.9 us: sent_to_all(): return lax.all_to_all(copies, axis, split_axis=0, concat_axis=0, tiled=True)]
    dot_general x7 -> x0, matrix products: 38.5 us -> none  [the longest x3 16.7 us: market_terms(): jnp.einsum('mjr,mr->mj', choice_prob, type_weight, precision=lax.Precisio...]
    gather x6 -> x0, local copies, waits for them, and re-layouts: 26.5 us -> none  [the longest x3 19 us: market_terms(): jnp.take(table, row_ids, axis=0)]
    reduce_sum x17 -> x0, other arithmetic: 19.8 us -> none  [the longest x2 8.09 us: market_terms(): choice_prob = expu / (1.0 + jnp.sum(expu, axis=1, keepdims=True))]
    broadcast_in_dim x16 -> x0, local copies, waits for them, and re-layouts: 12.6 us -> none  [the longest x14 12.4 us: sent_to_all(): copies = jnp.broadcast_to(array, (lax.axis_size(axis), *array.shape))]
  transfers between devices with their start and end apart: 8 -> 0, of which waited for: 6 -> 0; matrix products, arithmetic and copies ran while one was open for 10% -> 0% of each run, Pallas kernels for 0% -> 0%
where the time goes in v1:
time: 130 us; the launch traced here: 129 us
  Pallas kernels  116 us (89%)
  local copies, waits for them, and re-layouts  9.24 us (7%)
  other arithmetic  3.36 us (3%)
    pallas_call x1, Pallas kernels, local(): pl.pallas_call(functools.partial(kernel, dims), name='contraction', out_s...  116 us
    unnamed x8, local copies, waits for them, and re-layouts  5.43 us

profile of v1, /device:TPU:1, one launch (start us, length us, event | category | flops | bytes accessed | tf_op | source)
XLA Modules:
  0.0 129.3 jit_solution(3161309578813918914)
XLA Ops:
  0.6 0.0 copy-start
  0.6 1.3 %convert_element_type.7 = f32[512]{0:T(512)} convert(s32[512]{0:T(512)} %order_ref.1) | non-fusion elementwise | flops 512 | bytes 4096 | tf_op jit(solution)/shard_map/convert_element_type | solution.py:427
  1.9 0.7 convert_element_type.6
  2.6 0.1 reshape.42
  2.7 1.3 %copy.41.size_ref = f32[16,1]{1,0:T(8,128)} copy(f32[16,1]{0,1:T(1,128)} %bitcast.25) | data formatting | bytes 128 | tf_op jit(solution)/shard_map/reshape | solution.py:423
  4.0 0.1 copy.37
  4.1 0.1 copy.38
  4.2 0.1 broadcast_in_dim_reshape.7
  4.3 0.8 copy.33
  5.1 0.1 copy.34
  5.2 0.1 broadcast_in_dim_reshape.6
  5.3 0.8 copy.39
  6.1 0.1 copy.40
  6.2 0.7 reshape.44.share_ref
  6.8 0.9 copy.35
  7.7 0.7 multiply_bitcast_fusion
  8.5 0.2 copy.36
  8.7 0.2 reshape.40
  8.8 0.6 pad_maximum_fusion.pk_ref
  9.5 0.0 copy-done
  9.5 1.0 copy.42.draws_hbm
  10.4 116.0 %contraction.1 = (f32[8,128]{1,0:T(8,128)}, f32[4,1024]{1,0:T(4,128)}) custom-call(f32[8,8,128]{2,1,0:T(8,128)} %pad_maximum_fusion.pk_ref, f32[8,128]{1,0:T(8,128)} %reshape.44.share_ref, f32[16,1]{1,0:T(8,128)} %copy.41.size_ref, f32[16,1024]{1,0:T(8,128)} %weight_ref.1, f32[4,1024]{1,0:T(4,128)} %loy_ref.1, s32[512]{0:T(512)} %order_ref.1, ...), custom_call_target="tpu_custom_call" | custom-call | tf_op jit(solution)/shard_map/contraction/pallas_call | solution.py:401
  126.5 0.8 reshape.47
  127.2 0.1 copy.43
  127.3 0.7 copy.44
  128.0 1.3 %copy.46 = f32[4,1024]{1,0:T(4,128)} copy(f32[4,1024]{1,0:T(4,128)} %get-tuple-element.13) | data formatting | bytes 32768
Async XLA Ops:
  0.6 8.8 %copy-start = (f32[16,5,1024]{2,0,1:T(8,128)S(1)}, f32[16,5,1024]{2,0,1:T(8,128)}, u32[]{:S(2)}) copy-start(f32[16,5,1024]{2,0,1:T(8,128)} %param.14) | copy-start | bytes 983044

commit v2 on v1

v2 whole, which is shorter than its diff:
```python
import functools

import jax
import jax.numpy as jnp
from jax import lax
from jax.experimental import pallas as pl
from jax.experimental.pallas import tpu as pltpu
from jax.sharding import Mesh
from jax.sharding import PartitionSpec as P

ITERS = 3
CLIP_TARGET = 0.5
NORM_EPS = 1e-06
AXES = ("mkt_0", "mkt_1", "mkt_2", "grp")
MESH = pl.DeviceIdType.MESH
F32 = jnp.float32
BF16 = jnp.bfloat16
PK, SHOCK, LOY, TABLE, TMASS, OUT, PER_STEP = 0, 1, 2, 3, 4, 5, 6
PRED, RS, DMEAN, AG, SQ_G, SQ_H = 0, 1, 2, 3, 4, 5


def split_hi_lo(value):
    hi = value.astype(BF16)
    lo = (value - hi.astype(F32)).astype(BF16)
    return hi, lo


def kernel(
    dims,
    mean_ref,
    share_ref,
    firm_ref,
    traits_ref,
    scale_ref,
    size_ref,
    weight_ref,
    loy_ref,
    order_ref,
    order_row_ref,
    draws_hbm,
    fshare_hbm,
    mean_out,
    loy_out,
    square,
    pk_own,
    pk,
    shock_own,
    shock,
    fshare,
    fs_own,
    order_row_b,
    order_col_b,
    loy_in,
    own_table,
    table,
    tmass_s,
    tmass_r,
    lane_mask,
    traits_l,
    shocks_r,
    onehot,
    onehot_t,
    util,
    gsum,
    weighted_a,
    weighted_b,
    terms,
    acc,
    part,
    rs,
    pred,
    pred_r,
    dmean,
    dmean_s,
    gap_s,
    ag,
    sq_s,
    sq_r,
    sq2_s,
    sq2_r,
    loy_s,
    loc_sem,
    send,
    recv,
    recv_pk,
    recv_shock,
):
    nx, nz, nc, ny, mdev, ntraits, firms, draws_all, own = dims
    nh = nc * ny
    ng = nx * nz
    rows = firms // ng
    mrows = mdev * 64
    x, z, c, y = (lax.axis_index(a) for a in AXES)
    g = x * nz + z
    h = c * ny + y
    dys = (0, 1, 3, 2)
    hpeers = [(i % nc, dys[i // nc]) for i in range(1, nh)]
    far = {0: 0, 1: 1, 2: 2, 3: 1}
    gpeers = [(dx, dz) for dx in range(nx) for dz in range(nz) if (dx, dz) != (0, 0)]
    gpeers.sort(key=lambda d: -far[d[0]] - far[d[1]])

    def hdev(dc, dy):
        return lax.rem(c + dc, nc), lax.rem(y + dy, ny)

    def gdev(dx, dz):
        return lax.rem(x + dx, nx), lax.rem(z + dz, nz)

    def source(i):
        q = i // nc
        dy = q + q // 2 - 2 * (q // 3)
        return lax.rem(c + lax.rem(i, nc), nc) * ny + lax.rem(y + dy, ny)

    def lanes(index):
        return pl.ds(pl.multiple_of(index * 128, 128), 128)

    started = []

    def push(stage, src, dst, device, sem=None):
        pltpu.make_async_remote_copy(
            src_ref=src,
            dst_ref=dst,
            send_sem=send.at[stage],
            recv_sem=recv.at[stage] if sem is None else sem,
            device_id=device,
            device_id_type=MESH,
        ).start()

    def to_h(stage, src_of, dst, sems=None):
        for dc, dy in hpeers:
            c2, y2 = hdev(dc, dy)
            slot = dc + nc * dys.index((ny - dy) % ny)
            sem = None if sems is None else sems.at[slot]
            push(stage, src_of(c2 * ny + y2), dst, (x, z, c2, y2), sem)

    def to_g(stage, src_of, dst_of):
        for dx, dz in gpeers:
            x2, z2 = gdev(dx, dz)
            push(stage, src_of(x2 * nz + z2), dst_of(dx * nz + dz), (x2, z2, c, y))

    def arrived(stage, like):
        started.append((stage, like))
        pltpu.make_async_copy(like, like, recv.at[stage]).wait()

    def keep(src, dst, sem):
        copy = pltpu.make_async_copy(src, dst, sem)
        copy.start()
        return copy

    get_draws = keep(draws_hbm, shock_own.at[pl.ds(0, ntraits)], loc_sem.at[0])
    get_share = keep(fshare_hbm.at[:, lanes(h)], fshare, loc_sem.at[1])

    barrier = pltpu.get_barrier_semaphore()
    for dc, dy in hpeers:
        c2, y2 = hdev(dc, dy)
        pl.semaphore_signal(barrier, inc=1, device_id=(x, z, c2, y2), device_id_type=MESH)
    for dx, dz in gpeers:
        x2, z2 = gdev(dx, dz)
        pl.semaphore_signal(barrier, inc=1, device_id=(x2, z2, c, y), device_id_type=MESH)

    lane = lax.broadcasted_iota(jnp.int32, (8, 128), 1)
    lane16 = lax.broadcasted_iota(jnp.int32, (mdev, 128), 1)
    market = lax.broadcasted_iota(jnp.int32, (mdev, 128), 0)

    square[...] = jnp.zeros(square.shape, F32)
    for k in range(ntraits):
        square[k * mdev : (k + 1) * mdev, 0:64] = traits_ref[k] * scale_ref[k]
    mean_a = mean_ref[...].astype(BF16).astype(F32)
    ids = firm_ref[...].astype(F32) - 256.0
    square[5 * mdev : 6 * mdev, 0:64] = mean_a
    square[6 * mdev : 7 * mdev, 0:64] = ids
    square[7 * mdev : 8 * mdev, 0:64] = mean_ref[...] - mean_a
    pk_own[0:64, :] = square[...].T[0:64, :]
    for p in range(mdev // 2):
        even = square[6 * mdev + 2 * p : 6 * mdev + 2 * p + 1, :]
        odd = square[6 * mdev + 2 * p + 1 : 6 * mdev + 2 * p + 2, :]
        pk_own[64 + p : 65 + p, :] = even + pltpu.roll(odd, 64, 1)

    row_mass = None
    for m in range(mdev):
        shock_own[ntraits, m : m + 1, :] = weight_ref[m : m + 1, :] * size_ref[m]
    row_mass = jnp.sum(shock_own[ntraits], axis=1, keepdims=True)
    denom = jnp.sum(
        jnp.where(lax.rem(lane16, mdev) == market, row_mass, 0.0), axis=0, keepdims=True
    )

    pl.semaphore_wait(barrier, len(hpeers) + len(gpeers))

    to_h(LOY, lambda h2: loy_ref.at[:, lanes(h2)], loy_in.at[h])
    keep_loy = keep(loy_ref.at[:, lanes(h)], loy_in.at[h], loc_sem.at[2])
    to_h(PK, lambda h2: pk_own, pk.at[h], recv_pk)
    keep(pk_own, pk.at[h], recv_pk.at[0])
    get_draws.wait()
    to_h(SHOCK, lambda h2: shock_own.at[:, :, lanes(h2)], shock.at[h], recv_shock)
    keep(shock_own.at[:, :, lanes(h)], shock.at[h], recv_shock.at[0])
    started.append((PK, pk.at[pl.ds(0, nh - 1)]))
    started.append((SHOCK, shock.at[pl.ds(0, nh - 1)]))

    square[0:mdev, 0:64] = share_ref[...]
    turned = square[...].T
    log_share = jnp.zeros((8, 128), F32)
    for jb in range(8):
        block = turned[jb * 8 : jb * 8 + 8, :]
        if jb:
            block = pltpu.roll(block, jb * mdev, 1)
        log_share = jnp.where(lane // mdev == jb, block, log_share)
    log_share = jnp.log(log_share)
    order_f = order_row_ref[...].astype(F32) - 256.0
    order_row_b[...] = jnp.broadcast_to(order_f, order_row_b.shape).astype(BF16)
    for b in range(firms // 128):
        row = order_f[:, b * 128 : (b + 1) * 128]
        order_col_b[b * 128 : (b + 1) * 128, :] = jnp.broadcast_to(row, (128, 128)).T.astype(BF16)
    lane_b = lax.rem(lax.broadcasted_iota(jnp.int32, (16, 128), 1), mdev)
    for m in range(mdev):
        lane_mask[m] = jnp.where(lane_b == m, 1.0, 0.0).astype(BF16)
    kind = lax.broadcasted_iota(jnp.int32, (256, 256), 0) // mdev
    half = lax.broadcasted_iota(jnp.int32, (256, 256), 1) // 128
    kind = lax.rem(kind, 8)
    is_mean = jnp.logical_and(jnp.logical_or(kind == 5, kind == 7), half == 0)
    shocks_r[...] = jnp.where(is_mean, 1.0, 0.0).astype(BF16)
    get_share.wait()
    for k in range(rows):
        fs_own[k : k + 1, :] = fshare[pl.ds(order_ref[g * rows + k], 1), :]
    fs_own[...] = jnp.log(fs_own[...])

    keep_loy.wait()
    arrived(LOY, loy_in.at[pl.ds(0, nh - 1)])
    for hh in range(nh):
        own_table[hh * own : (hh + 1) * own, :] = loy_in[hh]
    to_g(TABLE, lambda g2: own_table, lambda slot: table.at[g])
    keep_own = keep(own_table, table.at[g], loc_sem.at[3])

    def build(i, carry):
        hh = source(i)
        pltpu.make_async_copy(pk.at[hh], pk.at[hh], recv_pk.at[i]).wait()
        base = pl.multiple_of(hh * mrows, mrows)
        one = jnp.ones((16, 128), BF16)
        zero = jnp.zeros((16, 128), BF16)
        for m in range(mdev):
            for b in range(4):
                at = 6 * mdev + m
                low = jnp.broadcast_to(pk[hh, b * 16 : b * 16 + 8, at : at + 1], (8, 128))
                high = jnp.broadcast_to(pk[hh, b * 16 + 8 : b * 16 + 16, at : at + 1], (8, 128))
                col = jnp.concatenate([low, high], axis=0).astype(BF16)
                for t in range(firms // 128):
                    hot = jnp.where(col == order_row_b[:, t * 128 : (t + 1) * 128], one, zero)
                    where = pl.ds(pl.multiple_of(base + m * 64 + b * 16, 16), 16)
                    onehot[where, t * 128 : (t + 1) * 128] = hot
        for p in range(mdev // 2):
            row = jnp.broadcast_to(pk[hh, 64 + p : 65 + p, :], (16, 128)).astype(BF16)
            for t in range(firms // 16):
                hot = jnp.where(order_col_b[t * 16 : t * 16 + 16, :] == row, one, zero)
                onehot_t[hh, t * 16 : t * 16 + 16, p * 128 : (p + 1) * 128] = hot
        return carry

    lax.fori_loop(0, nh, build, 0)

    keep_own.wait()
    arrived(TABLE, table.at[pl.ds(0, ng - 1)])

    def set_terms(source):
        hi, lo = split_hi_lo(source[...].reshape(firms, 128))
        terms[:, :128] = hi
        terms[:, 128:] = lo

    set_terms(table)

    def first(i, carry):
        hh = source(i)
        pltpu.make_async_copy(shock.at[hh], shock.at[hh], recv_shock.at[i]).wait()
        hi, lo = split_hi_lo(shock[hh, 0:ntraits].reshape(ntraits * mdev, 128))
        for part_of in range(2):
            at = part_of * 128
            shocks_r[at : at + ntraits * mdev, :128] = hi
            shocks_r[at : at + ntraits * mdev, 128:] = lo
        hi, lo = split_hi_lo(pk[hh, 0:64, :])
        for m in range(mdev):
            mask = lane_mask[m]
            for b in range(4):
                at = m * 64 + b * 16
                traits_l[at : at + 16, :128] = hi[b * 16 : b * 16 + 16] * mask
                traits_l[at : at + 16, 128:] = lo[b * 16 : b * 16 + 16] * mask
        base = pl.multiple_of(hh * mrows, mrows)
        both = jnp.dot(
            onehot[pl.ds(base, mrows), :], terms[...], preferred_element_type=F32
        ) + jnp.dot(traits_l[...], shocks_r[...], preferred_element_type=F32)
        util[pl.ds(base, mrows), :] = both[:, :128] + both[:, 128:]
        return carry

    lax.fori_loop(0, nh, first, 0)

    tm = jnp.sum(shock[:, ntraits].reshape(nh * mdev, 128), axis=0, keepdims=True)
    tmass_s[...] = tm
    to_g(TMASS, lambda g2: tmass_s, lambda slot: tmass_r.at[slot])

    delta_sum = jnp.zeros((8, 128), F32)
    type_mass = None
    clip = None
    own_new = own_table[...]

    for step in range(ITERS):
        stage = PER_STEP + 6 * step

        if step:
            def gather(hh, carry, step=step):
                base = pl.multiple_of(hh * mrows, mrows)
                both = jnp.dot(
                    onehot[pl.ds(base, mrows), :], terms[...], preferred_element_type=F32
                )
                gsum[pl.ds(base, mrows), :] = both[:, :128] + both[:, 128:]
                cols = dmean[step - 1, hh]
                for m in range(mdev):
                    for jb in range(8):
                        where = pl.ds(pl.multiple_of(base + m * 64 + jb * 8, 8), 8)
                        at = jb * mdev + m
                        util[where, :] = util[where, :] + cols[:, at : at + 1]
                return carry

            set_terms(ag.at[step - 1])
            lax.fori_loop(0, nh, gather, 0)
            arrived(stage - 6 + SQ_H, sq2_r.at[step - 1, pl.ds(0, nh - 1)])
            sq = jnp.sum(jnp.sum(sq2_r[step - 1], axis=0), axis=1, keepdims=True)
            clip = jnp.minimum(
                1.0, CLIP_TARGET / jnp.sqrt(sq / (firms * draws_all) + NORM_EPS)
            )
            own_new = own_new + clip * gap

        def choices(hh, weighted, step=step, clip=clip):
            base = pl.multiple_of(hh * mrows, mrows)
            compact = jnp.zeros((8, 128), F32)
            for m in range(mdev):
                expu = []
                total = None
                for jb in range(8):
                    where = pl.ds(pl.multiple_of(base + m * 64 + jb * 8, 8), 8)
                    u = util[where, :]
                    if step:
                        u = u + clip * gsum[where, :]
                        if step < ITERS - 1:
                            util[where, :] = u
                    e = jnp.exp(u)
                    expu.append(e)
                    total = e if total is None else total + e
                total = jnp.sum(total, axis=0, keepdims=True)
                scale = shock[hh, ntraits, m : m + 1, :] / (1.0 + total)
                for jb in range(0, 8, 2):
                    at = m * 64 + jb * 8
                    wts = [expu[jb] * scale, expu[jb + 1] * scale]
                    for k in range(2):
                        red = jnp.sum(wts[k], axis=1, keepdims=True)
                        compact = jnp.where(lane == (jb + k) * mdev + m, red, compact)
                    hi, lo = split_hi_lo(jnp.concatenate(wts, axis=0))
                    weighted[at : at + 16, :128] = hi
                    weighted[at : at + 16, 128:] = lo
            pred[step, hh] = compact

        def collect(hh, weighted):
            acc[...] = acc[...] + jnp.dot(
                onehot_t[hh], weighted[...], preferred_element_type=F32
            )

        def two_blocks(q, carry):
            collect(jnp.maximum(2 * q - 1, 0), weighted_b)
            choices(2 * q, weighted_a)
            collect(2 * q, weighted_a)
            choices(2 * q + 1, weighted_b)
            return carry

        acc[...] = jnp.zeros(acc.shape, F32)
        weighted_b[...] = jnp.zeros(weighted_b.shape, BF16)
        lax.fori_loop(0, nh // 2, two_blocks, 0)

        to_h(stage + PRED, lambda h2: pred.at[step, h2], pred_r.at[step, h])
        last = jnp.dot(onehot_t[nh - 1], weighted_b[...], preferred_element_type=F32)
        last = acc[...] + last
        part[step] = (last[:, :128] + last[:, 128:]).reshape(ng, rows, 128)
        to_g(stage + RS, lambda g2: part.at[step, g2], lambda slot: rs.at[step, slot - 1])

        arrived(stage + PRED, pred_r.at[step, pl.ds(0, nh - 1)])
        pred_r[step, h] = pred[step, h]
        num = jnp.sum(pred_r[step], axis=0)
        delta = log_share - jnp.log(num / denom)
        delta_sum = delta_sum + delta
        if step < ITERS - 1:
            dmean_s[step] = delta
            dmean[step, h] = delta
            to_h(stage + DMEAN, lambda h2: dmean_s.at[step], dmean.at[step, h])
        if step == 0:
            arrived(TMASS, tmass_r.at[pl.ds(1, ng - 1)])
            type_mass = tmass_s[...]
            for slot in range(1, ng):
                type_mass = type_mass + tmass_r[slot]

        arrived(stage + RS, rs.at[step])
        totals = part[step, g]
        for slot in range(ng - 1):
            totals = totals + rs[step, slot]
        gap = fs_own[...] - jnp.log(totals / type_mass)
        sq = jnp.sum(gap * gap, axis=0, keepdims=True)
        sq_s[step] = sq
        sq_r[step, 0] = sq
        to_g(stage + SQ_G, lambda g2: sq_s.at[step], lambda slot: sq_r.at[step, slot])
        if step < ITERS - 1:
            gap_s[step] = gap
            ag[step, g] = gap
            to_g(stage + AG, lambda g2: gap_s.at[step], lambda slot: ag.at[step, g])
        arrived(stage + SQ_G, sq_r.at[step, pl.ds(1, ng - 1)])
        sq = jnp.sum(sq_r[step], axis=0)
        sq2_s[step] = sq
        sq2_r[step, h] = sq
        to_h(stage + SQ_H, lambda h2: sq2_s.at[step], sq2_r.at[step, h])
        if step < ITERS - 1:
            arrived(stage + DMEAN, dmean.at[step, pl.ds(0, nh - 1)])
            arrived(stage + AG, ag.at[step, pl.ds(0, ng - 1)])

    square[0:8, :] = delta_sum
    turned = square[...].T
    natural = jnp.zeros((mdev, 128), F32)
    for jb in range(8):
        block = turned[jb * mdev : (jb + 1) * mdev, :]
        if jb:
            block = pltpu.roll(block, jb * 8, 1)
        natural = jnp.where(lane16 // 8 == jb, block, natural)
    mean_out[...] = mean_ref[...] + natural[:, 0:64]
    stage = PER_STEP + 6 * (ITERS - 1)
    arrived(stage + SQ_H, sq2_r.at[ITERS - 1, pl.ds(0, nh - 1)])
    sq = jnp.sum(jnp.sum(sq2_r[ITERS - 1], axis=0), axis=1, keepdims=True)
    clip = jnp.minimum(1.0, CLIP_TARGET / jnp.sqrt(sq / (firms * draws_all) + NORM_EPS))
    own_new = own_new + clip * gap
    for hh in range(nh):
        loy_s[hh] = own_new[hh * own : (hh + 1) * own, :]
    to_h(OUT, lambda h2: loy_s.at[h2], loy_out.at[:, lanes(h)])
    keep_out = keep(loy_s.at[h], loy_out.at[:, lanes(h)], loc_sem.at[4])
    keep_out.wait()
    arrived(OUT, loy_out.at[:, pl.ds(0, 128 * (nh - 1))])
    for stage, like in started:
        pltpu.make_async_copy(like, like, send.at[stage]).wait()


def local(
    mean_utility,
    market_share,
    product_traits,
    taste_draws,
    taste_scale,
    type_weight,
    market_size,
    product_firm,
    firm_order,
    loyalty,
    firm_share,
    shape,
):
    nx, nz, nc, ny = shape
    nh, ng = nc * ny, nx * nz
    mdev, ntraits, draws_all = taste_draws.shape
    firms = firm_share.shape[0]
    own = loyalty.shape[0]
    rows = firms // ng
    dims = (nx, nz, nc, ny, mdev, ntraits, firms, draws_all, own)
    vmem = pl.BlockSpec(memory_space=pltpu.VMEM)
    smem = pl.BlockSpec(memory_space=pltpu.SMEM)
    anywhere = pl.BlockSpec(memory_space=pl.ANY)
    scratch = [
        ((128, 128), F32),
        ((72, 128), F32),
        ((nh, 72, 128), F32),
        ((ntraits + 1, mdev, draws_all), F32),
        ((nh, ntraits + 1, mdev, 128), F32),
        ((firms, 128), F32),
        ((rows, 128), F32),
        ((16, firms), BF16),
        ((firms, 128), BF16),
        ((nh, own, 128), F32),
        ((rows, 128), F32),
        ((ng, rows, 128), F32),
        ((1, 128), F32),
        ((ng, 1, 128), F32),
        ((mdev, 16, 128), BF16),
        ((mdev * 64, 256), BF16),
        ((256, 256), BF16),
        ((nh * mdev * 64, firms), BF16),
        ((nh, firms, mdev * 64), BF16),
        ((nh * mdev * 64, 128), F32),
        ((nh * mdev * 64, 128), F32),
        ((mdev * 64, 256), BF16),
        ((mdev * 64, 256), BF16),
        ((firms, 256), BF16),
        ((firms, 256), F32),
        ((ITERS, ng, rows, 128), F32),
        ((ITERS, ng - 1, rows, 128), F32),
        ((ITERS, nh, 8, 128), F32),
        ((ITERS, nh, 8, 128), F32),
        ((ITERS - 1, nh, 8, 128), F32),
        ((ITERS - 1, 8, 128), F32),
        ((ITERS - 1, rows, 128), F32),
        ((ITERS - 1, ng, rows, 128), F32),
        ((ITERS, 1, 128), F32),
        ((ITERS, ng, 1, 128), F32),
        ((ITERS, 1, 128), F32),
        ((ITERS, nh, 1, 128), F32),
        ((nh, own, 128), F32),
    ]
    stages = PER_STEP + 6 * ITERS
    return pl.pallas_call(
        functools.partial(kernel, dims),
        name="contraction",
        out_shape=(
            jax.ShapeDtypeStruct((mdev, 64), F32),
            jax.ShapeDtypeStruct((own, draws_all), F32),
        ),
        in_specs=[vmem, vmem, vmem, vmem, smem, smem, vmem, vmem, smem, vmem, anywhere, anywhere],
        out_specs=(vmem, vmem),
        scratch_shapes=[pltpu.VMEM(s, d) for s, d in scratch]
        + [
            pltpu.SemaphoreType.DMA((5,)),
            pltpu.SemaphoreType.DMA((stages,)),
            pltpu.SemaphoreType.DMA((stages,)),
            pltpu.SemaphoreType.DMA((nh,)),
            pltpu.SemaphoreType.DMA((nh,)),
        ],
        compiler_params=pltpu.CompilerParams(
            collective_id=0, has_side_effects=True, vmem_limit_bytes=60 * 1024 * 1024
        ),
    )(
        mean_utility,
        market_share,
        product_firm,
        product_traits.transpose(2, 0, 1),
        taste_scale,
        market_size,
        type_weight,
        loyalty,
        firm_order,
        firm_order.reshape(1, firms),
        taste_draws.transpose(1, 0, 2),
        firm_share,
    )


def solution(mesh):
    shape = (4, 4, 2, mesh.shape["grp"])
    torus = Mesh(mesh.devices.reshape(shape), AXES)
    in_specs = (
        P(AXES, None),
        P(AXES, None),
        P(AXES, None, None),
        P(AXES, None, None),
        P(),
        P(AXES, None),
        P(AXES),
        P(AXES, None),
        P(),
        P(AXES, None),
        P(),
    )
    out_specs = (P(AXES, None), P(AXES, None))
    return jax.shard_map(
        functools.partial(local, shape=shape),
        mesh=torus,
        in_specs=in_specs,
        out_specs=out_specs,
        check_vma=False,
    )
```

time: 130 us -> 85.7 us (0.66)
  Pallas kernels: 116 us -> 82.1 us
  local copies, waits for them, and re-layouts: 9.24 us -> 2.62 us
  other arithmetic: 3.36 us -> 0 us
    pallas_call x1, Pallas kernels: 116 us -> 82.1 us  [local(): pl.pallas_call(functools.partial(kernel, dims), name='contraction', out_s...]
    reshape x5 -> x0, local copies, waits for them, and re-layouts: 3.03 us -> none  [the longest x1 1.33 us: local(): market_size.reshape(mdev, 1)]
    unnamed x8 -> x2, local copies, waits for them, and re-layouts: 5.43 us -> 2.62 us
    convert_element_type x2 -> x0, other arithmetic: 2.01 us -> none  [the longest x1 1.31 us: local(): firm_order.astype(F32).reshape(1, firms)]
where the time goes in v2:
time: 85.7 us; the launch traced here: 85.4 us
  Pallas kernels  82.1 us (96%)
  local copies, waits for them, and re-layouts  2.62 us (3%)
    pallas_call x1, Pallas kernels, local(): pl.pallas_call(functools.partial(kernel, dims), name='contraction', out_s...  82.1 us
    unnamed x2, local copies, waits for them, and re-layouts  2.62 us

profile of v2, /device:TPU:1, one launch (start us, length us, event | category | flops | bytes accessed | tf_op | source)
XLA Modules:
  0.0 85.4 jit_solution(16731056427122452316)
XLA Ops:
  0.6 82.1 %contraction.1 = (f32[16,64]{1,0:T(8,128)}, f32[4,1024]{1,0:T(4,128)}) custom-call(f32[16,64]{1,0:T(8,128)} %mean_ref.1, f32[16,64]{1,0:T(8,128)} %share_ref.1, s32[16,64]{1,0:T(8,128)} %firm_ref.1, f32[5,16,64]{2,1,0:T(8,128)} %bitcast.4, f32[5]{0:T(128)} %scale_ref.1, f32[16]{0:T(128)} %size_ref.1, f32[16,1024]{1,0:T(8,128)} %weight_ref.1, ...), custom_call_target="tpu_custom_call" | custom-call | tf_op jit(solution)/shard_map/contraction/pallas_call | solution.py:504
  82.8 1.3 %copy.15 = f32[16,64]{1,0:T(8,128)} copy(f32[16,64]{1,0:T(8,128)} %get-tuple-element.4) | data formatting | bytes 8192
  84.1 1.3 %copy.16 = f32[4,1024]{1,0:T(4,128)} copy(f32[4,1024]{1,0:T(4,128)} %get-tuple-element.5) | data formatting | bytes 32768

commit v3 on v2

v3 whole, which is shorter than its diff:
```python
import functools

import jax
import jax.numpy as jnp
from jax import lax
from jax.experimental import pallas as pl
from jax.experimental.pallas import tpu as pltpu
from jax.sharding import Mesh
from jax.sharding import PartitionSpec as P

ITERS = 3
CLIP_TARGET = 0.5
NORM_EPS = 1e-06
AXES = ("mkt_0", "mkt_1", "mkt_2", "grp")
MESH = pl.DeviceIdType.MESH
F32 = jnp.float32
BF16 = jnp.bfloat16
PK, SHOCK, LOY, TABLE, TMASS, OUT, PER_STEP = 0, 1, 2, 3, 4, 5, 6
PRED, RS, DMEAN, SQ_G, SQ_H, AG, STEP_STAGES = 0, 1, 2, 3, 4, 5, 6
LOG2E = 1.4426950408889634


def split_hi_lo(value):
    hi = value.astype(BF16)
    lo = (value - hi.astype(F32)).astype(BF16)
    return hi, lo


def kernel(
    dims,
    mean_ref,
    share_ref,
    firm_ref,
    traits_ref,
    scale_ref,
    size_ref,
    weight_ref,
    loy_ref,
    order_ref,
    order_row_ref,
    draws_hbm,
    fshare_hbm,
    mean_out,
    loy_out,
    square,
    pk_own,
    pk,
    shock_own,
    shock,
    fshare,
    fs_own,
    order_row_b,
    order_col_b,
    loy_in,
    own_table,
    table,
    tmass_s,
    tmass_r,
    lane_mask,
    traits_l,
    shocks_r,
    onehot,
    onehot_t,
    util,
    gsum,
    weighted_0,
    weighted_1,
    weighted_2,
    weighted_3,
    terms,
    acc,
    part,
    rs,
    pred,
    pred_r,
    dmean,
    dmean_s,
    gap_s,
    ag,
    sq_s,
    sq_r,
    sq2_s,
    sq2_r,
    fin_s,
    fin,
    loc_sem,
    send,
    recv,
    recv_pk,
    recv_shock,
):
    nx, nz, nc, ny, mdev, ntraits, firms, draws_all, own = dims
    weighted = (weighted_0, weighted_1, weighted_2, weighted_3)
    nh = nc * ny
    ng = nx * nz
    rows = firms // ng
    mrows = mdev * 64
    x, z, c, y = (lax.axis_index(a) for a in AXES)
    g = x * nz + z
    h = c * ny + y
    dys = (0, 1, 3, 2)
    hpeers = [(i % nc, dys[i // nc]) for i in range(1, nh)]
    far = {0: 0, 1: 1, 2: 2, 3: 1}
    gpeers = [(dx, dz) for dx in range(nx) for dz in range(nz) if (dx, dz) != (0, 0)]
    gpeers.sort(key=lambda d: -far[d[0]] - far[d[1]])

    def hdev(dc, dy):
        return lax.rem(c + dc, nc), lax.rem(y + dy, ny)

    def gdev(dx, dz):
        return lax.rem(x + dx, nx), lax.rem(z + dz, nz)

    def source(i):
        q = i // nc
        dy = q + q // 2 - 2 * (q // 3)
        return lax.rem(c + lax.rem(i, nc), nc) * ny + lax.rem(y + dy, ny)

    def lanes(index):
        return pl.ds(pl.multiple_of(index * 128, 128), 128)

    started = []

    def push(stage, src, dst, device, sem=None):
        pltpu.make_async_remote_copy(
            src_ref=src,
            dst_ref=dst,
            send_sem=send.at[stage],
            recv_sem=recv.at[stage] if sem is None else sem,
            device_id=device,
            device_id_type=MESH,
        ).start()

    def to_h(stage, src_of, dst, sems=None):
        for dc, dy in hpeers:
            c2, y2 = hdev(dc, dy)
            slot = dc + nc * dys.index((ny - dy) % ny)
            sem = None if sems is None else sems.at[slot]
            push(stage, src_of(c2 * ny + y2), dst, (x, z, c2, y2), sem)

    def to_g(stage, src_of, dst_of):
        for dx, dz in gpeers:
            x2, z2 = gdev(dx, dz)
            push(stage, src_of(x2 * nz + z2), dst_of(dx * nz + dz), (x2, z2, c, y))

    def arrived(stage, like):
        started.append((stage, like))
        pltpu.make_async_copy(like, like, recv.at[stage]).wait()

    def keep(src, dst, sem):
        copy = pltpu.make_async_copy(src, dst, sem)
        copy.start()
        return copy

    get_draws = keep(draws_hbm, shock_own.at[pl.ds(0, ntraits)], loc_sem.at[0])
    get_share = keep(fshare_hbm.at[:, lanes(h)], fshare, loc_sem.at[1])

    barrier = pltpu.get_barrier_semaphore()
    for dc, dy in hpeers:
        c2, y2 = hdev(dc, dy)
        pl.semaphore_signal(barrier, inc=1, device_id=(x, z, c2, y2), device_id_type=MESH)
    for dx, dz in gpeers:
        x2, z2 = gdev(dx, dz)
        pl.semaphore_signal(barrier, inc=1, device_id=(x2, z2, c, y), device_id_type=MESH)

    lane = lax.broadcasted_iota(jnp.int32, (8, 128), 1)
    lane_jb, lane_m = lane // mdev, lax.rem(lane, mdev)
    lane16 = lax.broadcasted_iota(jnp.int32, (mdev, 128), 1)
    market = lax.broadcasted_iota(jnp.int32, (mdev, 128), 0)

    square[...] = jnp.zeros(square.shape, F32)
    for k in range(ntraits):
        square[k * mdev : (k + 1) * mdev, 0:64] = traits_ref[k] * (scale_ref[k] * LOG2E)
    mean_2 = mean_ref[...] * LOG2E
    mean_a = mean_2.astype(BF16).astype(F32)
    ids = firm_ref[...].astype(F32) - 256.0
    square[5 * mdev : 6 * mdev, 0:64] = mean_a
    square[6 * mdev : 7 * mdev, 0:64] = ids
    square[7 * mdev : 8 * mdev, 0:64] = mean_2 - mean_a
    pk_own[0:64, :] = square[...].T[0:64, :]
    for p in range(mdev // 2):
        even = square[6 * mdev + 2 * p : 6 * mdev + 2 * p + 1, :]
        odd = square[6 * mdev + 2 * p + 1 : 6 * mdev + 2 * p + 2, :]
        pk_own[64 + p : 65 + p, :] = even + pltpu.roll(odd, 64, 1)

    row_mass = None
    for m in range(mdev):
        shock_own[ntraits, m : m + 1, :] = weight_ref[m : m + 1, :] * size_ref[m]
    row_mass = jnp.sum(shock_own[ntraits], axis=1, keepdims=True)
    denom = jnp.sum(
        jnp.where(lax.rem(lane16, mdev) == market, row_mass, 0.0), axis=0, keepdims=True
    )

    order_f = order_row_ref[...].astype(F32) - 256.0
    for b in range(firms // 128):
        row = order_f[:, b * 128 : (b + 1) * 128]
        order_row_b[b] = jnp.broadcast_to(row, (16, 128)).astype(BF16)
        order_col_b[b * 128 : (b + 1) * 128, :] = jnp.broadcast_to(row, (128, 128)).T.astype(BF16)
    lane_b = lax.rem(lax.broadcasted_iota(jnp.int32, (16, 128), 1), mdev)
    for m in range(mdev):
        lane_mask[m] = jnp.where(lane_b == m, 1.0, 0.0).astype(BF16)
    kind = lax.rem(lax.broadcasted_iota(jnp.int32, (256, 128), 0) // mdev, 8)
    is_mean = jnp.logical_or(kind == 5, kind == 7)
    shocks_r[0] = jnp.where(is_mean, 1.0, 0.0).astype(BF16)
    shocks_r[1] = jnp.zeros((256, 128), BF16)

    def joined(ref):
        return jnp.concatenate([ref[k] for k in range(ref.shape[0])], axis=1)

    def folded(both):
        return both[:, :128] + both[:, 128:]

    def build(i, carry):
        hh = source(i)
        pltpu.make_async_copy(pk.at[hh], pk.at[hh], recv_pk.at[i]).wait()
        base = pl.multiple_of(hh * mrows, mrows)
        one = jnp.ones((16, 128), BF16)
        zero = jnp.zeros((16, 128), BF16)
        for m in range(mdev):
            at = 6 * mdev + m
            for b in range(4):
                col = jnp.broadcast_to(pk[hh, b * 16 : b * 16 + 16, at : at + 1], (16, 128))
                col = col.astype(BF16)
                where = pl.ds(pl.multiple_of(base + m * 64 + b * 16, 16), 16)
                for t in range(firms // 128):
                    onehot[t, where, :] = jnp.where(col == order_row_b[t], one, zero)
        for p in range(mdev // 2):
            row = jnp.broadcast_to(pk[hh, 64 + p : 65 + p, :], (16, 128)).astype(BF16)
            for t in range(firms // 16):
                at = t * 16
                hot = jnp.where(order_col_b[at : at + 16, :] == row, one, zero)
                onehot_t[hh, p, at : at + 16, :] = hot
        return carry

    def tastes(i, carry):
        hh = source(i)
        pltpu.make_async_copy(shock.at[hh], shock.at[hh], recv_shock.at[i]).wait()
        hi, lo = split_hi_lo(shock[hh, 0:ntraits].reshape(ntraits * mdev, 128))
        for part_of in range(2):
            at = part_of * 128
            shocks_r[0, at : at + ntraits * mdev, :] = hi
            shocks_r[1, at : at + ntraits * mdev, :] = lo
        hi, lo = split_hi_lo(pk[hh, 0:64, :])
        for m in range(mdev):
            mask = lane_mask[m]
            for b in range(4):
                at = m * 64 + b * 16
                traits_l[0, at : at + 16, :] = hi[b * 16 : b * 16 + 16] * mask
                traits_l[1, at : at + 16, :] = lo[b * 16 : b * 16 + 16] * mask
        base = pl.multiple_of(hh * mrows, mrows)
        both = jnp.dot(joined(traits_l), joined(shocks_r), preferred_element_type=F32)
        util[pl.ds(base, mrows), :] = folded(both)
        return carry

    def set_terms(source):
        hi, lo = split_hi_lo(source[...].reshape(firms, 128) * LOG2E)
        terms[0] = hi
        terms[1] = lo

    def gather():
        chunk = nh * mrows // 2

        def block(q, carry):
            where = pl.ds(pl.multiple_of(q * chunk, chunk), chunk)
            hot = jnp.concatenate([onehot[t, where, :] for t in range(firms // 128)], axis=1)
            both = jnp.dot(hot, joined(terms), preferred_element_type=F32)
            gsum[where, :] = folded(both)
            return carry

        lax.fori_loop(0, 2, block, 0)

    keep(pk_own, pk.at[h], recv_pk.at[0])
    get_draws.wait()
    keep(shock_own.at[:, :, lanes(h)], shock.at[h], recv_shock.at[0])
    build(0, 0)

    pl.semaphore_wait(barrier, len(hpeers) + len(gpeers))

    to_h(LOY, lambda h2: loy_ref.at[:, lanes(h2)], loy_in.at[h])
    keep_loy = keep(loy_ref.at[:, lanes(h)], loy_in.at[h], loc_sem.at[2])
    to_h(PK, lambda h2: pk_own, pk.at[h], recv_pk)
    to_h(SHOCK, lambda h2: shock_own.at[:, :, lanes(h2)], shock.at[h], recv_shock)
    started.append((PK, pk.at[pl.ds(0, nh - 1)]))
    started.append((SHOCK, shock.at[pl.ds(0, nh - 1)]))

    square[0:mdev, 0:64] = share_ref[...]
    turned = square[...].T
    log_share = jnp.zeros((8, 128), F32)
    for jb in range(8):
        block = turned[jb * 8 : jb * 8 + 8, :]
        if jb:
            block = pltpu.roll(block, jb * mdev, 1)
        log_share = jnp.where(lane // mdev == jb, block, log_share)
    log_share = jnp.log(log_share)
    get_share.wait()
    for k in range(rows):
        fs_own[k : k + 1, :] = fshare[pl.ds(order_ref[g * rows + k], 1), :]
    fs_own[...] = jnp.log(fs_own[...])
    tastes(0, 0)
    build(1, 0)

    keep_loy.wait()
    arrived(LOY, loy_in.at[pl.ds(0, nh - 1)])
    for hh in range(nh):
        own_table[hh * own : (hh + 1) * own, :] = loy_in[hh]
    to_g(TABLE, lambda g2: own_table, lambda slot: table.at[g])
    keep_own = keep(own_table, table.at[g], loc_sem.at[3])

    lax.fori_loop(2, nh, build, 0)
    lax.fori_loop(1, nh, tastes, 0)
    keep_own.wait()
    arrived(TABLE, table.at[pl.ds(0, ng - 1)])
    set_terms(table)
    gather()
    tm = jnp.sum(shock[:, ntraits].reshape(nh * mdev, 128), axis=0, keepdims=True)
    tmass_s[...] = tm
    to_g(TMASS, lambda g2: tmass_s, lambda slot: tmass_r.at[slot])

    delta_sum = jnp.zeros((8, 128), F32)
    type_mass = None
    clip = None

    def clip_of(step):
        sq = jnp.sum(jnp.sum(sq2_r[step], axis=0), axis=1, keepdims=True)
        return jnp.minimum(1.0, CLIP_TARGET / jnp.sqrt(sq / (firms * draws_all) + NORM_EPS))

    own_new = own_table[...]

    for step in range(ITERS):
        stage = PER_STEP + STEP_STAGES * step

        if step:
            before = stage - STEP_STAGES
            arrived(before + SQ_H, sq2_r.at[step - 1, pl.ds(0, nh - 1)])
            clip = clip_of(step - 1)
            own_new = own_new + clip * gap

        def choices(hh, weighted, step=step, clip=clip):
            base = pl.multiple_of(hh * mrows, mrows)
            compact = jnp.zeros((8, 128), F32)
            for m in range(mdev):
                expu = []
                total = None
                for jb in range(8):
                    where = pl.ds(pl.multiple_of(base + m * 64 + jb * 8, 8), 8)
                    moved = gsum[where, :]
                    u = util[where, :] + (clip * moved if step else moved)
                    if step < ITERS - 1:
                        util[where, :] = u
                    e = jnp.exp2(u)
                    expu.append(e)
                    total = e if total is None else total + e
                total = jnp.sum(total, axis=0, keepdims=True)
                scale = shock[hh, ntraits, m : m + 1, :] / (1.0 + total)
                reds = None
                for jb in range(0, 8, 2):
                    at = m * 64 + jb * 8
                    wts = [expu[jb] * scale, expu[jb + 1] * scale]
                    for k in range(2):
                        red = jnp.sum(wts[k], axis=1, keepdims=True)
                        reds = red if reds is None else jnp.where(lane_jb == jb + k, red, reds)
                    hi, lo = split_hi_lo(jnp.concatenate(wts, axis=0))
                    weighted[0, at : at + 16, :] = hi
                    weighted[1, at : at + 16, :] = lo
                compact = jnp.where(lane_m == m, reds, compact)
            pred[step, hh] = compact

        def collected(hh, weighted):
            return jnp.dot(joined(onehot_t.at[hh]), joined(weighted), preferred_element_type=F32)

        def four_blocks(q, carry):
            sums = collected(jnp.maximum(4 * q - 1, 0), weighted[3])
            for k in range(4):
                choices(4 * q + k, weighted[k])
                if k < 3:
                    sums = sums + collected(4 * q + k, weighted[k])
            acc[...] = acc[...] + sums
            return carry

        acc[...] = jnp.zeros(acc.shape, F32)
        weighted[3][...] = jnp.zeros(weighted[3].shape, BF16)
        lax.fori_loop(0, nh // 4, four_blocks, 0)

        last = acc[...] + collected(nh - 1, weighted[3])
        part[step] = (last[:, :128] + last[:, 128:]).reshape(ng, rows, 128)
        to_g(stage + RS, lambda g2: part.at[step, g2], lambda slot: rs.at[step, slot - 1])
        to_h(stage + PRED, lambda h2: pred.at[step, h2], pred_r.at[step, h])

        arrived(stage + PRED, pred_r.at[step, pl.ds(0, nh - 1)])
        pred_r[step, h] = pred[step, h]
        num = jnp.sum(pred_r[step], axis=0)
        delta = log_share - jnp.log(num / denom)
        delta_sum = delta_sum + delta
        if step < ITERS - 1:
            dmean_s[step] = delta * LOG2E
            dmean[step, h] = delta * LOG2E
            to_h(stage + DMEAN, lambda h2: dmean_s.at[step], dmean.at[step, h])
        if step == 0:
            arrived(TMASS, tmass_r.at[pl.ds(1, ng - 1)])
            type_mass = tmass_s[...]
            for slot in range(1, ng):
                type_mass = type_mass + tmass_r[slot]

        arrived(stage + RS, rs.at[step])
        totals = part[step, g]
        for slot in range(ng - 1):
            totals = totals + rs[step, slot]
        gap = fs_own[...] - jnp.log(totals / type_mass)
        sq = jnp.sum(gap * gap, axis=0, keepdims=True)
        sq_s[step] = sq
        sq_r[step, 0] = sq
        to_g(stage + SQ_G, lambda g2: sq_s.at[step], lambda slot: sq_r.at[step, slot])
        if step < ITERS - 1:
            gap_s[step] = gap
            ag[step, g] = gap
            to_g(stage + AG, lambda g2: gap_s.at[step], lambda slot: ag.at[step, g])
            arrived(stage + DMEAN, dmean.at[step, pl.ds(0, nh - 1)])

            def shift(hh, carry, step=step):
                base = pl.multiple_of(hh * mrows, mrows)
                cols = dmean[step, hh]
                for m in range(mdev):
                    for jb in range(8):
                        where = pl.ds(pl.multiple_of(base + m * 64 + jb * 8, 8), 8)
                        at = jb * mdev + m
                        util[where, :] = util[where, :] + cols[:, at : at + 1]
                return carry

            lax.fori_loop(0, nh, shift, 0)
        else:
            for hh in range(nh):
                fin_s[hh, 0] = own_new[hh * own : (hh + 1) * own, :]
                fin_s[hh, 1] = gap[hh * own : (hh + 1) * own, :]
            to_h(OUT, lambda h2: fin_s.at[h2], fin.at[h])
            keep_out = keep(fin_s.at[h], fin.at[h], loc_sem.at[4])
            square[0:8, :] = delta_sum
            turned = square[...].T
            natural = jnp.zeros((mdev, 128), F32)
            for jb in range(8):
                block = turned[jb * mdev : (jb + 1) * mdev, :]
                if jb:
                    block = pltpu.roll(block, jb * 8, 1)
                natural = jnp.where(lane16 // 8 == jb, block, natural)
            mean_out[...] = mean_ref[...] + natural[:, 0:64]
        arrived(stage + SQ_G, sq_r.at[step, pl.ds(1, ng - 1)])
        sq = jnp.sum(sq_r[step], axis=0)
        sq2_s[step] = sq
        sq2_r[step, h] = sq
        to_h(stage + SQ_H, lambda h2: sq2_s.at[step], sq2_r.at[step, h])
        if step < ITERS - 1:
            arrived(stage + AG, ag.at[step, pl.ds(0, ng - 1)])
            set_terms(ag.at[step])
            gather()

    keep_out.wait()
    arrived(OUT, fin.at[pl.ds(0, nh - 1)])
    stage = PER_STEP + STEP_STAGES * (ITERS - 1)
    for at, like in started:
        pltpu.make_async_copy(like, like, send.at[at]).wait()
    arrived(stage + SQ_H, sq2_r.at[ITERS - 1, pl.ds(0, nh - 1)])
    clip = clip_of(ITERS - 1)
    for hh in range(nh):
        loy_out[:, hh * 128 : (hh + 1) * 128] = fin[hh, 0] + clip * fin[hh, 1]
    like = sq2_r.at[ITERS - 1, pl.ds(0, nh - 1)]
    pltpu.make_async_copy(like, like, send.at[stage + SQ_H]).wait()


def handed_on(mean_ref, loy_ref, mean_out, loy_out):
    mean_out[...] = mean_ref[...]
    loy_out[...] = loy_ref[...]


def local(
    mean_utility,
    market_share,
    product_traits,
    taste_draws,
    taste_scale,
    type_weight,
    market_size,
    product_firm,
    firm_order,
    loyalty,
    firm_share,
    shape,
):
    nx, nz, nc, ny = shape
    nh, ng = nc * ny, nx * nz
    mdev, ntraits, draws_all = taste_draws.shape
    firms = firm_share.shape[0]
    own = loyalty.shape[0]
    rows = firms // ng
    dims = (nx, nz, nc, ny, mdev, ntraits, firms, draws_all, own)
    vmem = pl.BlockSpec(memory_space=pltpu.VMEM)
    smem = pl.BlockSpec(memory_space=pltpu.SMEM)
    anywhere = pl.BlockSpec(memory_space=pl.ANY)
    scratch = [
        ((128, 128), F32),
        ((72, 128), F32),
        ((nh, 72, 128), F32),
        ((ntraits + 1, mdev, draws_all), F32),
        ((nh, ntraits + 1, mdev, 128), F32),
        ((firms, 128), F32),
        ((rows, 128), F32),
        ((firms // 128, 16, 128), BF16),
        ((firms, 128), BF16),
        ((nh, own, 128), F32),
        ((rows, 128), F32),
        ((ng, rows, 128), F32),
        ((1, 128), F32),
        ((ng, 1, 128), F32),
        ((mdev, 16, 128), BF16),
        ((2, mdev * 64, 128), BF16),
        ((2, 256, 128), BF16),
        ((firms // 128, nh * mdev * 64, 128), BF16),
        ((nh, mdev // 2, firms, 128), BF16),
        ((nh * mdev * 64, 128), F32),
        ((nh * mdev * 64, 128), F32),
        ((2, mdev * 64, 128), BF16),
        ((2, mdev * 64, 128), BF16),
        ((2, mdev * 64, 128), BF16),
        ((2, mdev * 64, 128), BF16),
        ((2, firms, 128), BF16),
        ((firms, 256), F32),
        ((ITERS, ng, rows, 128), F32),
        ((ITERS, ng - 1, rows, 128), F32),
        ((ITERS, nh, 8, 128), F32),
        ((ITERS, nh, 8, 128), F32),
        ((ITERS - 1, nh, 8, 128), F32),
        ((ITERS - 1, 8, 128), F32),
        ((ITERS - 1, rows, 128), F32),
        ((ITERS - 1, ng, rows, 128), F32),
        ((ITERS, 1, 128), F32),
        ((ITERS, ng, 1, 128), F32),
        ((ITERS, 1, 128), F32),
        ((ITERS, nh, 1, 128), F32),
        ((nh, 2, own, 128), F32),
        ((nh, 2, own, 128), F32),
    ]
    stages = PER_STEP + STEP_STAGES * ITERS
    results = pl.pallas_call(
        functools.partial(kernel, dims),
        name="contraction",
        out_shape=(
            jax.ShapeDtypeStruct((mdev, 64), F32),
            jax.ShapeDtypeStruct((own, draws_all), F32),
        ),
        in_specs=[vmem, vmem, vmem, vmem, smem, smem, vmem, vmem, smem, vmem, anywhere, anywhere],
        out_specs=(vmem, vmem),
        scratch_shapes=[pltpu.VMEM(s, d) for s, d in scratch]
        + [
            pltpu.SemaphoreType.DMA((5,)),
            pltpu.SemaphoreType.DMA((stages,)),
            pltpu.SemaphoreType.DMA((stages,)),
            pltpu.SemaphoreType.DMA((nh,)),
            pltpu.SemaphoreType.DMA((nh,)),
        ],
        compiler_params=pltpu.CompilerParams(
            collective_id=0, has_side_effects=True, vmem_limit_bytes=60 * 1024 * 1024
        ),
    )(
        mean_utility,
        market_share,
        product_firm,
        product_traits.transpose(2, 0, 1),
        taste_scale,
        market_size,
        type_weight,
        loyalty,
        firm_order,
        firm_order.reshape(1, firms),
        taste_draws.transpose(1, 0, 2),
        firm_share,
    )
    return pl.pallas_call(
        handed_on,
        name="handed_on",
        out_shape=tuple(jax.ShapeDtypeStruct(r.shape, F32) for r in results),
        in_specs=[vmem, vmem],
        out_specs=(vmem, vmem),
    )(*results)


def solution(mesh):
    shape = (4, 4, 2, mesh.shape["grp"])
    torus = Mesh(mesh.devices.reshape(shape), AXES)
    in_specs = (
        P(AXES, None),
        P(AXES, None),
        P(AXES, None, None),
        P(AXES, None, None),
        P(),
        P(AXES, None),
        P(AXES),
        P(AXES, None),
        P(),
        P(AXES, None),
        P(),
    )
    out_specs = (P(AXES, None), P(AXES, None))
    return jax.shard_map(
        functools.partial(local, shape=shape),
        mesh=torus,
        in_specs=in_specs,
        out_specs=out_specs,
        check_vma=False,
    )
```

time: 85.7 us -> 77.4 us (0.903)
  Pallas kernels: 82.1 us -> 76.5 us
  local copies, waits for them, and re-layouts: 2.62 us -> 0 us
    pallas_call x1, Pallas kernels: 82.1 us -> 75.2 us  [local(): pl.pallas_call(functools.partial(kernel, dims), name='contraction', out_s...]
    unnamed x2 -> x0, local copies, waits for them, and re-layouts: 2.62 us -> none
    pallas_call x0 -> x1, Pallas kernels: none -> 1.35 us  [local(): pl.pallas_call(handed_on, name='handed_on', out_shape=tuple((jax.ShapeDty...]
where the time goes in v3:
time: 77.4 us; the launch traced here: 77.2 us
  Pallas kernels  76.5 us (99%)
    pallas_call x1, Pallas kernels, local(): pl.pallas_call(functools.partial(kernel, dims), name='contraction', out_s...  75.2 us

profile of v3, /device:TPU:1, one launch (start us, length us, event | category | flops | bytes accessed | tf_op | source)
XLA Modules:
  0.0 77.2 jit_solution(541770843512829169)
XLA Ops:
  0.6 75.2 %contraction.1 = (f32[16,64]{1,0:T(8,128)}, f32[4,1024]{1,0:T(4,128)}) custom-call(f32[16,64]{1,0:T(8,128)} %mean_ref.1, f32[16,64]{1,0:T(8,128)} %share_ref.1, s32[16,64]{1,0:T(8,128)} %firm_ref.1, f32[5,16,64]{2,1,0:T(8,128)} %bitcast.4, f32[5]{0:T(128)} %scale_ref.1, f32[16]{0:T(128)} %size_ref.1, f32[16,1024]{1,0:T(8,128)} %weight_ref.1, ...), custom_call_target="tpu_custom_call" | custom-call | tf_op jit(solution)/shard_map/contraction/pallas_call | solution.py:540
  75.8 1.3 %handed_on.1 = (f32[16,64]{1,0:T(8,128)}, f32[4,1024]{1,0:T(4,128)}) custom-call(f32[16,64]{1,0:T(8,128)} %get-tuple-element.4.mean_ref, f32[4,1024]{1,0:T(4,128)} %get-tuple-element.5.loy_ref), custom_call_target="tpu_custom_call" | custom-call | tf_op jit(solution)/shard_map/handed_on/pallas_call | solution.py:574

commit v4 on v3

--- a/solution.py
+++ b/solution.py
@@ -28,20 +28,30 @@
 
 def kernel(
     dims,
+    mean_hbm,
+    share_hbm,
+    firm_hbm,
+    traits_hbm,
+    scale_hbm,
+    size_hbm,
+    weight_hbm,
+    loy_hbm,
+    order_hbm,
+    order_row_hbm,
+    draws_hbm,
+    fshare_hbm,
+    mean_out,
+    loy_out,
     mean_ref,
     share_ref,
     firm_ref,
     traits_ref,
+    weight_ref,
+    loy_ref,
+    order_row_ref,
     scale_ref,
     size_ref,
-    weight_ref,
-    loy_ref,
     order_ref,
-    order_row_ref,
-    draws_hbm,
-    fshare_hbm,
-    mean_out,
-    loy_out,
     square,
     pk_own,
     pk,
@@ -151,9 +161,6 @@
         copy.start()
         return copy
 
-    get_draws = keep(draws_hbm, shock_own.at[pl.ds(0, ntraits)], loc_sem.at[0])
-    get_share = keep(fshare_hbm.at[:, lanes(h)], fshare, loc_sem.at[1])
-
     barrier = pltpu.get_barrier_semaphore()
     for dc, dy in hpeers:
         c2, y2 = hdev(dc, dy)
@@ -162,11 +169,33 @@
         x2, z2 = gdev(dx, dz)
         pl.semaphore_signal(barrier, inc=1, device_id=(x2, z2, c, y), device_id_type=MESH)
 
+    fetched = [
+        keep(src, dst, loc_sem.at[5 + k])
+        for k, (src, dst) in enumerate(
+            [
+                (traits_hbm, traits_ref),
+                (mean_hbm, mean_ref),
+                (firm_hbm, firm_ref),
+                (order_row_hbm, order_row_ref),
+                (weight_hbm, weight_ref),
+                (loy_hbm, loy_ref),
+                (share_hbm, share_ref),
+                (scale_hbm, scale_ref),
+                (size_hbm, size_ref),
+                (order_hbm, order_ref),
+            ]
+        )
+    ]
+    get_draws = keep(draws_hbm, shock_own.at[pl.ds(0, ntraits)], loc_sem.at[0])
+    get_share = keep(fshare_hbm.at[:, lanes(h)], fshare, loc_sem.at[1])
+
     lane = lax.broadcasted_iota(jnp.int32, (8, 128), 1)
     lane_jb, lane_m = lane // mdev, lax.rem(lane, mdev)
     lane16 = lax.broadcasted_iota(jnp.int32, (mdev, 128), 1)
     market = lax.broadcasted_iota(jnp.int32, (mdev, 128), 0)
 
+    for copy in fetched:
+        copy.wait()
     square[...] = jnp.zeros(square.shape, F32)
     for k in range(ntraits):
         square[k * mdev : (k + 1) * mdev, 0:64] = traits_ref[k] * (scale_ref[k] * LOG2E)
@@ -491,9 +520,15 @@
     rows = firms // ng
     dims = (nx, nz, nc, ny, mdev, ntraits, firms, draws_all, own)
     vmem = pl.BlockSpec(memory_space=pltpu.VMEM)
-    smem = pl.BlockSpec(memory_space=pltpu.SMEM)
     anywhere = pl.BlockSpec(memory_space=pl.ANY)
     scratch = [
+        ((mdev, 64), F32),
+        ((mdev, 64), F32),
+        ((mdev, 64), jnp.int32),
+        ((ntraits, mdev, 64), F32),
+        ((mdev, draws_all), F32),
+        ((own, draws_all), F32),
+        ((1, firms), jnp.int32),
         ((128, 128), F32),
         ((72, 128), F32),
         ((nh, 72, 128), F32),
@@ -544,11 +579,17 @@
             jax.ShapeDtypeStruct((mdev, 64), F32),
             jax.ShapeDtypeStruct((own, draws_all), F32),
         ),
-        in_specs=[vmem, vmem, vmem, vmem, smem, smem, vmem, vmem, smem, vmem, anywhere, anywhere],
+        in_specs=[anywhere] * 12,
         out_specs=(vmem, vmem),
-        scratch_shapes=[pltpu.VMEM(s, d) for s, d in scratch]
+        scratch_shapes=[pltpu.VMEM(s, d) for s, d in scratch[:7]]
         + [
-            pltpu.SemaphoreType.DMA((5,)),
+            pltpu.SMEM((ntraits,), F32),
+            pltpu.SMEM((mdev,), F32),
+            pltpu.SMEM((firms,), jnp.int32),
+        ]
+        + [pltpu.VMEM(s, d) for s, d in scratch[7:]]
+        + [
+            pltpu.SemaphoreType.DMA((15,)),
             pltpu.SemaphoreType.DMA((stages,)),
             pltpu.SemaphoreType.DMA((stages,)),
             pltpu.SemaphoreType.DMA((nh,)),

time: 77.4 us -> 76.3 us (0.986)
  Pallas kernels: 76.5 us -> 75.5 us
    pallas_call x1, Pallas kernels: 75.2 us -> 74.2 us  [local(): pl.pallas_call(functools.partial(kernel, dims), name='contraction', out_s...]
where the time goes in v4:
time: 76.3 us; the launch traced here: 76.2 us
  Pallas kernels  75.5 us (99%)
    pallas_call x1, Pallas kernels, local(): pl.pallas_call(functools.partial(kernel, dims), name='contraction', out_s...  74.2 us

profile of v4, /device:TPU:1, one launch (start us, length us, event | category | flops | bytes accessed | tf_op | source)
XLA Modules:
  0.0 76.2 jit_solution(531250670769107430)
XLA Ops:
  0.6 74.2 %contraction.1 = (f32[16,64]{1,0:T(8,128)}, f32[4,1024]{1,0:T(4,128)}) custom-call(f32[16,64]{1,0:T(8,128)} %mean_hbm.1, f32[16,64]{1,0:T(8,128)} %share_hbm.1, s32[16,64]{1,0:T(8,128)} %firm_hbm.1, f32[5,16,64]{2,1,0:T(8,128)} %bitcast.4, f32[5]{0:T(128)} %scale_hbm.1, f32[16]{0:T(128)} %size_hbm.1, f32[16,1024]{1,0:T(8,128)} %weight_hbm.1, ...), custom_call_target="tpu_custom_call" | custom-call | tf_op jit(solution)/shard_map/contraction/pallas_call | solution.py:575
  74.8 1.3 %handed_on.1 = (f32[16,64]{1,0:T(8,128)}, f32[4,1024]{1,0:T(4,128)}) custom-call(f32[16,64]{1,0:T(8,128)} %get-tuple-element.4.mean_ref, f32[4,1024]{1,0:T(4,128)} %get-tuple-element.5.loy_ref), custom_call_target="tpu_custom_call" | custom-call | tf_op jit(solution)/shard_map/handed_on/pallas_call | solution.py:615

commit v5 on v4

--- a/solution.py
+++ b/solution.py
@@ -140,8 +140,10 @@
             device_id_type=MESH,
         ).start()
 
-    def to_h(stage, src_of, dst, sems=None):
+    def to_h(stage, src_of, dst, sems=None, only=None):
         for dc, dy in hpeers:
+            if only is not None and not only(dc, dy):
+                continue
             c2, y2 = hdev(dc, dy)
             slot = dc + nc * dys.index((ny - dy) % ny)
             sem = None if sems is None else sems.at[slot]
@@ -238,9 +240,16 @@
     def folded(both):
         return both[:, :128] + both[:, 128:]
 
-    def build(i, carry):
+    def build(i, carry, forward=None):
         hh = source(i)
         pltpu.make_async_copy(pk.at[hh], pk.at[hh], recv_pk.at[i]).wait()
+        if forward is not None:
+            partner = (x, z, lax.rem(c + 1, nc), y)
+
+            @pl.when(forward)
+            def _():
+                push(PK, pk.at[hh], pk.at[hh], partner, recv_pk.at[i + 1])
+
         base = pl.multiple_of(hh * mrows, mrows)
         one = jnp.ones((16, 128), BF16)
         zero = jnp.zeros((16, 128), BF16)
@@ -306,7 +315,7 @@
 
     to_h(LOY, lambda h2: loy_ref.at[:, lanes(h2)], loy_in.at[h])
     keep_loy = keep(loy_ref.at[:, lanes(h)], loy_in.at[h], loc_sem.at[2])
-    to_h(PK, lambda h2: pk_own, pk.at[h], recv_pk)
+    to_h(PK, lambda h2: pk_own, pk.at[h], recv_pk, lambda dc, dy: dc == 0 or dy == 0)
     to_h(SHOCK, lambda h2: shock_own.at[:, :, lanes(h2)], shock.at[h], recv_shock)
     started.append((PK, pk.at[pl.ds(0, nh - 1)]))
     started.append((SHOCK, shock.at[pl.ds(0, nh - 1)]))
@@ -334,7 +343,12 @@
     to_g(TABLE, lambda g2: own_table, lambda slot: table.at[g])
     keep_own = keep(own_table, table.at[g], loc_sem.at[3])
 
-    lax.fori_loop(2, nh, build, 0)
+    others = ny - 1
+
+    def build_next(k, carry):
+        return build(2 + 2 * k - (2 * others - 1) * (k // others), carry, k < others)
+
+    lax.fori_loop(0, nh - 2, build_next, 0)
     lax.fori_loop(1, nh, tastes, 0)
     keep_own.wait()
     arrived(TABLE, table.at[pl.ds(0, ng - 1)])

time: 76.3 us -> 75.4 us (0.988)
  Pallas kernels: 75.5 us -> 74.6 us
    pallas_call x1, Pallas kernels: 74.2 us -> 73.2 us  [local(): pl.pallas_call(functools.partial(kernel, dims), name='contraction', out_s...]
where the time goes in v5:
time: 75.4 us; the launch traced here: 75.2 us
  Pallas kernels  74.6 us (99%)
    pallas_call x1, Pallas kernels, local(): pl.pallas_call(functools.partial(kernel, dims), name='contraction', out_s...  73.2 us

profile of v5, /device:TPU:1, one launch (start us, length us, event | category | flops | bytes accessed | tf_op | source)
XLA Modules:
  0.0 75.2 jit_solution(878877367174854392)
XLA Ops:
  0.6 73.2 %contraction.1 = (f32[16,64]{1,0:T(8,128)}, f32[4,1024]{1,0:T(4,128)}) custom-call(f32[16,64]{1,0:T(8,128)} %mean_hbm.1, f32[16,64]{1,0:T(8,128)} %share_hbm.1, s32[16,64]{1,0:T(8,128)} %firm_hbm.1, f32[5,16,64]{2,1,0:T(8,128)} %bitcast.4, f32[5]{0:T(128)} %scale_hbm.1, f32[16]{0:T(128)} %size_hbm.1, f32[16,1024]{1,0:T(8,128)} %weight_hbm.1, ...), custom_call_target="tpu_custom_call" | custom-call | tf_op jit(solution)/shard_map/contraction/pallas_call | solution.py:589
  73.9 1.3 %handed_on.1 = (f32[16,64]{1,0:T(8,128)}, f32[4,1024]{1,0:T(4,128)}) custom-call(f32[16,64]{1,0:T(8,128)} %get-tuple-element.4.mean_ref, f32[4,1024]{1,0:T(4,128)} %get-tuple-element.5.loy_ref), custom_call_target="tpu_custom_call" | custom-call | tf_op jit(solution)/shard_map/handed_on/pallas_call | solution.py:629
